TPU v7x, 32 devices: a whole 2x2x4 slice. The times are simulated.
32 devices in a mesh: parts: 2 (over y), sec: 16 (over z, x, core).
Axes of the slice: x: 2, y: 2, z: 4, core: 2. Of those that a mesh axis runs over, the one named last changes fastest.
Arguments:
- carry: bfloat16 [32, 96, 1152], P(('parts', 'sec')), parts along dimension 0, may hold values from -0.625 to 0.625
- site: bfloat16 [32, 96, 1536], P(('parts', 'sec')), parts along dimension 0, may hold values from -6 to 6
- mpo: bfloat16 [24, 16, 16, 12], P('parts'), parts along dimension 0, may hold values from -1.25 to 1.25
- omega: bfloat16 [1152, 128], replicated, may hold values from -0.1875 to 0.1875
- sector_sizes: int32 [32], P('parts'), parts along dimension 0, may hold values from 1 to 96, 768 in all
Outputs:
- left_factor: bfloat16 [32, 16, 96, 128], P(('parts', 'sec')), parts along dimension 0
- next_carry: bfloat16 [32, 128, 1152], P(('parts', 'sec')), parts along dimension 0
There are 2 independent parts, one for each index of `parts`. A program takes and returns all parts, laid end to end along the dimension named above; an argument that names none is the same for every part. Nothing has to cross between parts.
Inputs may be any that keep to these rules, and one draw needn't show every extreme that they name: `sector_sizes`: they sum to 768 and the largest is exactly 96.
All inputs are finite; a program needn't handle non-finite values.
Results may differ from a plain program's by a relative error of at most 0.0095.
Values may be sent and summed in bfloat16 or wider, within the bound.
A program may use at most 64 MiB of HBM per device.

v0:
```python
import jax
import jax.numpy as jnp
import numpy as np
from jax import lax
from jax.sharding import PartitionSpec as P

GRID_DN = 8


SPANS = ((-1, 0, 1), (0, 1, 3), (1, 3, 4))
GROUPS = ((0, 4, 0, 0), (4, 6, 1, 0), (6, 8, -1, 0), (8, 10, 0, 1), (10, 12, 0, -1))


def shifted(value, axis, steps):
    count = lax.axis_size(axis)
    initial, last = (max(0, -steps), min(count, count - steps))
    return lax.ppermute(value, axis, [(source, source + steps) for source in range(initial, last)])


def charge_tables():
    levels = np.array([-1, 0, 0, 1], np.int32)
    phys_up = np.repeat(levels, 4)
    phys_down = np.tile(levels, 4)
    bond_up = np.array([0, 0, 0, 0, 1, 1, -1, -1, 0, 0, 0, 0], np.int32)
    bond_down = np.array([0, 0, 0, 0, 0, 0, 0, 0, 1, 1, -1, -1], np.int32)
    return (phys_up, phys_down, bond_up, bond_down)


def conserving():
    phys_up, phys_down, bond_up, bond_down = charge_tables()
    left_up = bond_up[:, None, None, None] + phys_up[None, :, None, None]
    right_up = phys_up[None, None, :, None] + bond_up[None, None, None, :]
    left_down = bond_down[:, None, None, None] + phys_down[None, :, None, None]
    right_down = phys_down[None, None, :, None] + bond_down[None, None, None, :]
    return (left_up == right_up) & (left_down == right_down)


def inside(sector, shift_up, shift_down, count):
    upper = sector // GRID_DN + shift_up
    lower = sector % GRID_DN + shift_down
    return (upper >= 0) & (upper < count // GRID_DN) & (lower >= 0) & (lower < GRID_DN)


def orthonormal(sketch):
    gram = (
        jnp.dot(
            sketch.T, sketch, precision=lax.Precision.HIGHEST, preferred_element_type=jnp.float32
        )
        / sketch.shape[0]
    )
    ridge = 0.05 * jnp.trace(gram) / gram.shape[0] + 1e-06
    lower = jnp.linalg.cholesky(gram + ridge * jnp.eye(gram.shape[0], dtype=jnp.float32))
    solved = jax.scipy.linalg.solve_triangular(lower, sketch.T, lower=True)
    return solved.T.astype(jnp.bfloat16)


def shifted_site(block, offset):
    return shifted(block, "sec", offset)


def moved_rows(block, offset):
    return shifted(block, "sec", offset)


def body(carry, site, mpo, omega, sector_sizes):
    count = lax.axis_size("sec")
    sector = lax.axis_index("sec")
    capacity = carry.shape[1]
    bond_width = mpo.shape[0]
    phys_width = mpo.shape[1]
    phys_up, phys_down, bond_up, bond_down = charge_tables()
    rows = jnp.arange(capacity, dtype=jnp.int32)
    own_live = rows < sector_sizes[sector]
    targets = sector + jnp.asarray(phys_up * GRID_DN + phys_down)
    target_ok = inside(sector, phys_up, phys_down, count)
    target_sizes = sector_sizes[jnp.clip(targets, 0, count - 1)]
    column_live = target_ok[:, None] & (rows[None, :] < target_sizes[:, None])
    site_four = site[0].reshape(capacity, phys_width, capacity)
    site_masked = jnp.where(
        own_live[:, None, None] & column_live[None, :, :], site_four, jnp.zeros_like(site_four)
    )
    site_masked = site_masked.reshape(capacity, phys_width * capacity)
    carry_three = jnp.where(own_live[:, None], carry[0], jnp.zeros_like(carry[0])).reshape(
        capacity, bond_width, capacity
    )
    pieces = []
    for first_bond, last_bond, shift_up, shift_down in GROUPS:
        offset = shift_up * GRID_DN + shift_down
        source = site_masked if offset == 0 else shifted_site(site_masked, offset)
        valid = inside(sector, -shift_up, -shift_down, count)
        carry_part = carry_three[:, first_bond:last_bond]
        carry_part = jnp.where(valid, carry_part, jnp.zeros_like(carry_part))
        group_width = last_bond - first_bond
        product = jnp.dot(
            carry_part.reshape(capacity * group_width, capacity),
            source,
            preferred_element_type=jnp.float32,
        )
        pieces.append(product.reshape(capacity, group_width, phys_width * capacity))
    partial_sum = (
        jnp.concatenate(pieces, 1)
        .astype(jnp.bfloat16)
        .reshape(capacity, bond_width, phys_width, capacity)
    )
    operator = jnp.where(jnp.asarray(conserving()), mpo, jnp.zeros_like(mpo))
    joined = jnp.einsum(
        "awsb,wtsv->tavb", partial_sum, operator, preferred_element_type=jnp.float32
    )
    joined = jnp.where(target_ok[:, None, None, None], joined, 0.0).astype(jnp.bfloat16)
    blocks = joined.reshape(4, 4, capacity, bond_width * capacity)
    row_groups = []
    for shift_up, up_first, up_last in SPANS:
        pieces_row = []
        for shift_down, down_first, down_last in SPANS:
            part = blocks[up_first:up_last, down_first:down_last]
            offset = shift_up * GRID_DN + shift_down
            pieces_row.append(part if offset == 0 else moved_rows(part, offset))
        row_groups.append(jnp.concatenate(pieces_row, 1))
    gathered = jnp.concatenate(row_groups, 0)
    block = gathered.reshape(phys_width * capacity, bond_width * capacity)
    contract_rows = (((0,), (0,)), ((), ()))
    first_sketch = jnp.dot(block, omega, preferred_element_type=jnp.float32)
    basis = orthonormal(first_sketch)
    across = lax.dot_general(
        block, basis, contract_rows, preferred_element_type=jnp.float32
    ).astype(jnp.bfloat16)
    second_sketch = jnp.dot(block, across, preferred_element_type=jnp.float32)
    left_basis = orthonormal(second_sketch)
    projected = lax.dot_general(
        left_basis, block, contract_rows, preferred_element_type=jnp.float32
    )
    total = lax.psum(jnp.sum(projected * projected), "sec")
    next_carry = (projected * jnp.sqrt(count / total)).astype(jnp.bfloat16)
    return (left_basis.reshape(1, phys_width, capacity, left_basis.shape[1]), next_carry[None])


def solution(mesh):
    return jax.shard_map(
        body,
        mesh=mesh,
        in_specs=(
            P(("parts", "sec"), None, None),
            P(("parts", "sec"), None, None),
            P("parts", None, None, None),
            P(),
            P("parts"),
        ),
        out_specs=(P(("parts", "sec"), None, None, None), P(("parts", "sec"), None, None)),
        check_vma=False,
    )
```

profile of v0, /device:TPU:0, one launch (start us, length us, event | category | flops | bytes accessed | tf_op | source)
XLA Modules:
  0.0 228.1 jit_solution(12480270409447230724)
XLA Ops:
  7.5 6.0 %collective-permute-start = (bf16[96,1536]{1,0:T(8,128)(2,1)}, bf16[96,1536]{1,0:T(8,128)(2,1)S(1)}, u32[]{:S(2)}, u32[]{:S(2)}) collective-permute-start(bf16[96,1536]{1,0:T(8,128)(2,1)} %and_select_fusion), channel_id=1, source_target_pairs={{0,8},{1,9},{2,10},{3,11},{4,12},{5,13},{6,14},{7,15},{16,24},{17,... | collective-permute-start | bytes 884744 | tf_op jit(solution)/shard_map/ppermute | solution.py:17
  14.8 2.2 collective-permute-start.2
  23.2 8.2 %collective-permute-done.1 = bf16[96,1536]{1,0:T(8,128)(2,1)S(1)} collective-permute-done((bf16[96,1536]{1,0:T(8,128)(2,1)}, bf16[96,1536]{1,0:T(8,128)(2,1)S(1)}, u32[]{:S(2)}, u32[]{:S(2)}) %collective-permute-start.1) | collective-permute-done | bytes 294944 | tf_op jit(solution)/shard_map/ppermute | solution.py:17
  35.0 2.1 convolution_convert_fusion
  43.3 7.8 %fusion.1 = bf16[16,96,12,96]{3,0,1,2:T(8,128)(2,1)} fusion(pred[16]{0:T(512)(128)(4,1)S(1)} %compare_and_fusion.1, bf16[96,12,16,96]{3,0,2,1:T(8,128)(2,1)} %copy_dynamic-update-slice_fusion, pred[12,16,16,12]{2,1,3,0:T(8,128)(4,1)S(1)} %copy-done.3, bf16[12,16,16,12]{2,1,3,0:T(8,128)(2,1)S(1)} %copy-done.2), kind=kOutput, calls=%fused_computation.3 | convolution fusion | flops 683053056 | bytes 7188496 | tf_op jit(solution)/shard_map/awsb,wtsv->tavb/dot_general | solution.py:106
  51.1 7.1 %copy.71 = bf16[16,96,12,96]{1,3,2,0:T(8,128)(2,1)} copy(bf16[16,96,12,96]{3,0,1,2:T(8,128)(2,1)} %fusion.1) | data formatting | bytes 7077888 | tf_op jit(solution)/shard_map/convert_element_type | solution.py:109
  65.0 3.1 %collective-permute-start.8 = (bf16[2,1,96,1152]{3,2,1,0:T(8,128)(2,1)S(1)}, bf16[2,1,96,1152]{3,2,1,0:T(8,128)(2,1)S(1)}, u32[]{:S(2)}, u32[]{:S(2)}) collective-permute-start(bf16[2,1,96,1152]{3,2,1,0:T(8,128)(2,1)S(1)} %copy.75), channel_id=1, source_target_pairs={{0,1},{1,2},{2,3},{3,4},{4,5},{5,6},{6,7},{7,8},{8,9},{9,10},{10,1... | collective-permute-start | bytes 1327112 | tf_op jit(solution)/shard_map/ppermute | solution.py:17
  69.1 6.2 %collective-permute-start.10 = (bf16[1,2,96,1152]{3,2,1,0:T(8,128)(2,1)}, bf16[1,2,96,1152]{3,2,1,0:T(8,128)(2,1)}, u32[]{:S(2)}, u32[]{:S(2)}) collective-permute-start(bf16[1,2,96,1152]{3,2,1,0:T(8,128)(2,1)} %copy.78), channel_id=1, source_target_pairs={{0,8},{1,9},{2,10},{3,11},{4,12},{5,13},{6,14},{7,15},{16,24},{17,... | collective-permute-start | bytes 1327112 | tf_op jit(solution)/shard_map/ppermute | solution.py:17
  75.3 2.3 fusion.43
  79.5 3.1 %collective-permute-done.5 = bf16[1,2,96,1152]{3,2,1,0:T(8,128)(2,1)S(1)} collective-permute-done((bf16[1,2,96,1152]{3,2,1,0:T(8,128)(2,1)}, bf16[1,2,96,1152]{3,2,1,0:T(8,128)(2,1)S(1)}, u32[]{:S(2)}, u32[]{:S(2)}) %collective-permute-start.5) | collective-permute-done | bytes 442400 | tf_op jit(solution)/shard_map/ppermute | solution.py:17
  86.1 21.9 %collective-permute-start.9 = (bf16[1,1,96,1152]{2,3,1,0:T(8,128)(2,1)}, bf16[1,1,96,1152]{2,3,1,0:T(8,128)(2,1)}, u32[]{:S(2)}, u32[]{:S(2)}) collective-permute-start(bf16[1,1,96,1152]{2,3,1,0:T(8,128)(2,1)} %get-tuple-element.8), channel_id=1, source_target_pairs={{0,7},{1,8},{2,9},{3,10},{4,11},{5,12},{6,13},{7,14},{8,15},{16,23... | collective-permute-start | bytes 663560 | tf_op jit(solution)/shard_map/ppermute | solution.py:17
  111.3 2.1 copy.79
  114.2 4.9 %maximum_maximum_fusion = bf16[4,4,96,1152]{2,3,1,0:T(8,128)(2,1)} fusion(bf16[1,1,96,1152]{2,3,1,0:T(8,128)(2,1)} %collective-permute-done.11, bf16[1,2,96,1152]{2,3,1,0:T(8,128)(2,1)} %copy.79, bf16[1,1,96,1152]{2,3,1,0:T(8,128)(2,1)} %collective-permute-done.9, bf16[2,1,96,1152]{2,3,1,0:T(8,128)(2,1)S(1)} %copy.77, bf16[2,2,96,1152]{2,3,1,0:T(8,128)(2,1)S(1)} %slice.75, ...), kind=kLoop, calls=%fused_computation.4 | loop fusion | flops 14155776 | bytes 7077888 | tf_op jit(solution)/shard_map/concatenate | solution.py:119
  119.0 6.5 %copy.80 = bf16[4,4,96,1152]{3,2,1,0:T(8,128)(2,1)} copy(bf16[4,4,96,1152]{2,3,1,0:T(8,128)(2,1)} %maximum_maximum_fusion) | data formatting | bytes 7077888 | tf_op jit(solution)/shard_map/concatenate | solution.py:119
  125.5 3.1 %fusion.46 = f32[1536,128]{1,0:T(8,128)S(1)} fusion(bf16[1536,1152]{1,0:T(8,128)(2,1)} %bitcast.98, bf16[1152,128]{1,0:T(8,128)(2,1)S(1)} %copy-done), kind=kOutput, calls=%fused_computation.91 | convolution fusion | flops 452984832 | bytes 4620288 | tf_op jit(solution)/shard_map/dot_general | solution.py:122
  128.6 2.0 select_reduce_fusion.2
  131.4 11.7 %cholesky.44 = f32[128,128]{1,0:T(8,128)S(1)} custom-call(f32[128,128]{1,0:T(8,128)S(1)} %fusion.26), custom_call_target="Cholesky" | custom-call | tf_op jit(solution)/shard_map/jit(cholesky)/cholesky | solution.py:52
  144.4 9.8 %custom-call.6 = f32[1,128,128]{1,2,0:T(8,128)S(1)} custom-call(f32[1,128,128]{2,1,0:T(8,128)S(1)} %fusion.21), custom_call_target="InvertDiagBlocksLowerTriangular" | custom-call | tf_op jit(solution)/shard_map/jit(_solve_triangular)/triangular_solve | solution.py:53
  155.1 6.8 %fusion.8 = f32[1536,128]{1,0:T(8,128)S(1)} fusion(bf16[1536,1152]{1,0:T(8,128)(2,1)} %bitcast.99, bf16[128,1536]{1,0:T(8,128)(2,1)S(1)} %convolution_convert_fusion.6), kind=kOutput, calls=%fused_computation.19 | convolution fusion | flops 906117120 | bytes 4718592 | tf_op jit(solution)/shard_map/dot_general | solution.py:127
  161.9 2.2 select_reduce_fusion.1
  165.0 11.7 %cholesky.55 = f32[128,128]{1,0:T(8,128)S(1)} custom-call(f32[128,128]{1,0:T(8,128)S(1)} %fusion.24), custom_call_target="Cholesky" | custom-call | tf_op jit(solution)/shard_map/jit(cholesky)/cholesky | solution.py:52
  178.0 9.8 %custom-call.7 = f32[1,128,128]{1,2,0:T(8,128)S(1)} custom-call(f32[1,128,128]{2,1,0:T(8,128)S(1)} %fusion.22), custom_call_target="InvertDiagBlocksLowerTriangular" | custom-call | tf_op jit(solution)/shard_map/jit(_solve_triangular)/triangular_solve | solution.py:53
  188.7 3.3 %multiply_reduce_fusion = (f32[]{:T(128)}, f32[128,1152]{1,0:T(8,128)S(1)}) fusion(bf16[128,1536]{1,0:T(8,128)(2,1)S(1)} %convolution_convert_fusion.4, bf16[1536,1152]{1,0:T(8,128)(2,1)} %bitcast.100), kind=kOutput, calls=%fused_computation.28 | convolution fusion | flops 453279744 | bytes 4521988 | tf_op jit(solution)/shard_map/dot_general | solution.py:129
  192.0 33.7 %psum.7 = f32[]{:T(128)} all-reduce(f32[]{:T(128)} %get-tuple-element.18), channel_id=1, replica_groups=mesh['parts'=2,'sec'=16] {'sec'}, use_global_device_ids=true, to_apply=%region_5.8 | all-reduce | flops 1 | bytes 8 | tf_op jit(solution)/shard_map/psum | solution.py:132
  (82 shorter events, 47.5 us)
Async XLA Ops:
  0.6 124.8 %copy-start = (bf16[1152,128]{1,0:T(8,128)(2,1)S(1)}, bf16[1152,128]{1,0:T(8,128)(2,1)}, u32[]{:S(2)}) copy-start(bf16[1152,128]{1,0:T(8,128)(2,1)} %param.15) | copy-start | bytes 884740
  7.5 15.3 %collective-permute-start = (bf16[96,1536]{1,0:T(8,128)(2,1)}, bf16[96,1536]{1,0:T(8,128)(2,1)S(1)}, u32[]{:S(2)}, u32[]{:S(2)}) collective-permute-start(bf16[96,1536]{1,0:T(8,128)(2,1)} %and_select_fusion), channel_id=1, source_target_pairs={{0,8},{1,9},{2,10},{3,11},{4,12},{5,13},{6,14},{7,15},{16,24},{17,... | collective-permute-start | bytes 884744 | tf_op jit(solution)/shard_map/ppermute | solution.py:17
  13.5 17.9 %collective-permute-start.1 = (bf16[96,1536]{1,0:T(8,128)(2,1)}, bf16[96,1536]{1,0:T(8,128)(2,1)S(1)}, u32[]{:S(2)}, u32[]{:S(2)}) collective-permute-start(bf16[96,1536]{1,0:T(8,128)(2,1)} %and_select_fusion), channel_id=1, source_target_pairs={{8,0},{9,1},{10,2},{11,3},{12,4},{13,5},{14,6},{15,7},{24,16},{25,... | collective-permute-start | bytes 884744 | tf_op jit(solution)/shard_map/ppermute | solution.py:17
  14.8 18.2 %collective-permute-start.2 = (bf16[96,1536]{1,0:T(8,128)(2,1)}, bf16[96,1536]{1,0:T(8,128)(2,1)}, u32[]{:S(2)}, u32[]{:S(2)}) collective-permute-start(bf16[96,1536]{1,0:T(8,128)(2,1)} %and_select_fusion), channel_id=1, source_target_pairs={{0,1},{1,2},{2,3},{3,4},{4,5},{5,6},{6,7},{7,8},{8,9},{9,10},{10,1... | collective-permute-start | bytes 884744 | tf_op jit(solution)/shard_map/ppermute | solution.py:17
  17.0 18.0 %collective-permute-start.3 = (bf16[96,1536]{1,0:T(8,128)(2,1)}, bf16[96,1536]{1,0:T(8,128)(2,1)}, u32[]{:S(2)}, u32[]{:S(2)}) collective-permute-start(bf16[96,1536]{1,0:T(8,128)(2,1)} %and_select_fusion), channel_id=1, source_target_pairs={{1,0},{2,1},{3,2},{4,3},{5,4},{6,5},{7,6},{8,7},{9,8},{10,9},{11,1... | collective-permute-start | bytes 884744 | tf_op jit(solution)/shard_map/ppermute | solution.py:17
  38.9 4.4 %copy-start.2 = (bf16[12,16,16,12]{2,1,3,0:T(8,128)(2,1)S(1)}, bf16[12,16,16,12]{2,1,3,0:T(8,128)(2,1)}, u32[]{:S(2)}) copy-start(bf16[12,16,16,12]{2,1,3,0:T(8,128)(2,1)} %param.14) | copy-start | bytes 221188
  38.9 4.4 %copy-start.3 = (pred[12,16,16,12]{2,1,3,0:T(8,128)(4,1)S(1)}, pred[12,16,16,12]{2,1,3,0:T(8,128)(4,1)}, u32[]{:S(2)}) copy-start(pred[12,16,16,12]{2,1,3,0:T(8,128)(4,1)} %constant.136.clone) | copy-start | bytes 110596
  61.8 20.9 %collective-permute-start.5 = (bf16[1,2,96,1152]{3,2,1,0:T(8,128)(2,1)}, bf16[1,2,96,1152]{3,2,1,0:T(8,128)(2,1)S(1)}, u32[]{:S(2)}, u32[]{:S(2)}) collective-permute-start(bf16[1,2,96,1152]{3,2,1,0:T(8,128)(2,1)} %copy.72), channel_id=1, source_target_pairs={{8,0},{9,1},{10,2},{11,3},{12,4},{13,5},{14,6},{15,7},{24,16},{25,... | collective-permute-start | bytes 1327112 | tf_op jit(solution)/shard_map/ppermute | solution.py:17
  63.4 20.6 %collective-permute-start.7 = (bf16[2,1,96,1152]{3,2,1,0:T(8,128)(2,1)S(1)}, bf16[2,1,96,1152]{3,2,1,0:T(8,128)(2,1)S(1)}, u32[]{:S(2)}, u32[]{:S(2)}) collective-permute-start(bf16[2,1,96,1152]{3,2,1,0:T(8,128)(2,1)S(1)} %copy.74), channel_id=1, source_target_pairs={{1,0},{2,1},{3,2},{4,3},{5,4},{6,5},{7,6},{8,7},{9,8},{10,9},{11,1... | collective-permute-start | bytes 1327112 | tf_op jit(solution)/shard_map/ppermute | solution.py:17
  65.0 20.3 %collective-permute-start.8 = (bf16[2,1,96,1152]{3,2,1,0:T(8,128)(2,1)S(1)}, bf16[2,1,96,1152]{3,2,1,0:T(8,128)(2,1)S(1)}, u32[]{:S(2)}, u32[]{:S(2)}) collective-permute-start(bf16[2,1,96,1152]{3,2,1,0:T(8,128)(2,1)S(1)} %copy.75), channel_id=1, source_target_pairs={{0,1},{1,2},{2,3},{3,4},{4,5},{5,6},{6,7},{7,8},{8,9},{9,10},{10,1... | collective-permute-start | bytes 1327112 | tf_op jit(solution)/shard_map/ppermute | solution.py:17
  69.1 42.2 %collective-permute-start.10 = (bf16[1,2,96,1152]{3,2,1,0:T(8,128)(2,1)}, bf16[1,2,96,1152]{3,2,1,0:T(8,128)(2,1)}, u32[]{:S(2)}, u32[]{:S(2)}) collective-permute-start(bf16[1,2,96,1152]{3,2,1,0:T(8,128)(2,1)} %copy.78), channel_id=1, source_target_pairs={{0,8},{1,9},{2,10},{3,11},{4,12},{5,13},{6,14},{7,15},{16,24},{17,... | collective-permute-start | bytes 1327112 | tf_op jit(solution)/shard_map/ppermute | solution.py:17
  77.5 35.8 %collective-permute-start.11 = (bf16[1,1,96,1152]{2,3,1,0:T(8,128)(2,1)}, bf16[1,1,96,1152]{2,3,1,0:T(8,128)(2,1)}, u32[]{:S(2)}, u32[]{:S(2)}) collective-permute-start(bf16[1,1,96,1152]{2,3,1,0:T(8,128)(2,1)} %get-tuple-element.7), channel_id=1, source_target_pairs={{0,9},{1,10},{2,11},{3,12},{4,13},{5,14},{6,15},{16,25},{17,26},{1... | collective-permute-start | bytes 663560 | tf_op jit(solution)/shard_map/ppermute | solution.py:17
  82.7 30.7 %collective-permute-start.4 = (bf16[1,1,96,1152]{2,3,1,0:T(8,128)(2,1)}, bf16[1,1,96,1152]{2,3,1,0:T(8,128)(2,1)}, u32[]{:S(2)}, u32[]{:S(2)}) collective-permute-start(bf16[1,1,96,1152]{2,3,1,0:T(8,128)(2,1)} %get-tuple-element.6), channel_id=1, source_target_pairs={{9,0},{10,1},{11,2},{12,3},{13,4},{14,5},{15,6},{25,16},{26,17},{2... | collective-permute-start | bytes 663560 | tf_op jit(solution)/shard_map/ppermute | solution.py:17
  84.0 29.4 %collective-permute-start.6 = (bf16[1,1,96,1152]{2,3,1,0:T(8,128)(2,1)}, bf16[1,1,96,1152]{2,3,1,0:T(8,128)(2,1)S(1)}, u32[]{:S(2)}, u32[]{:S(2)}) collective-permute-start(bf16[1,1,96,1152]{2,3,1,0:T(8,128)(2,1)} %get-tuple-element.9), channel_id=1, source_target_pairs={{7,0},{8,1},{9,2},{10,3},{11,4},{12,5},{13,6},{14,7},{15,8},{23,16... | collective-permute-start | bytes 663560 | tf_op jit(solution)/shard_map/ppermute | solution.py:17
  85.3 0.8 copy-start.1
  86.1 28.1 %collective-permute-start.9 = (bf16[1,1,96,1152]{2,3,1,0:T(8,128)(2,1)}, bf16[1,1,96,1152]{2,3,1,0:T(8,128)(2,1)}, u32[]{:S(2)}, u32[]{:S(2)}) collective-permute-start(bf16[1,1,96,1152]{2,3,1,0:T(8,128)(2,1)} %get-tuple-element.8), channel_id=1, source_target_pairs={{0,7},{1,8},{2,9},{3,10},{4,11},{5,12},{6,13},{7,14},{8,15},{16,23... | collective-permute-start | bytes 663560 | tf_op jit(solution)/shard_map/ppermute | solution.py:17
where the time goes:
time: 229 us; the launch traced here: 228 us
  other arithmetic  56.5 us (25%)
  starting transfers between devices  49 us (21%)
  local copies, waits for them, and re-layouts  40.9 us (18%)
  blocking collectives  33.7 us (15%)
  matrix products  32.7 us (14%)
  waiting for transfers between devices  12.2 us (5%)
  between operations  3.12 us (1%)
    ppermute x12, starting transfers between devices, shifted(): lax.ppermute(value, axis, [(source, source + steps) for source in range(i...  49 us
    psum x1, blocking collectives, body(): total = lax.psum(jnp.sum(projected * projected), 'sec')  33.7 us
    another operation x6, other arithmetic, orthonormal(): jnp.linalg.cholesky(gram + ridge * jnp.eye(gram.shape[0], dtype=jnp.float...  24.8 us
    another operation x4, other arithmetic, orthonormal(): solved = jax.scipy.linalg.solve_triangular(lower, sketch.T, lower=True)  20.9 us
    ppermute x12, waiting for transfers between devices, shifted(): lax.ppermute(value, axis, [(source, source + steps) for source in range(i...  12.2 us
    slice x8, local copies, waits for them, and re-layouts, body(): part = blocks[up_first:up_last, down_first:down_last]  8.85 us
    dot_general x1, matrix products, body(): jnp.einsum('awsb,wtsv->tavb', partial_sum, operator, preferred_element_ty...  7.82 us
    convert_element_type x1, local copies, waits for them, and re-layouts, body(): jnp.where(target_ok[:, None, None, None], joined, 0.0).astype(jnp.bfloat16)  7.05 us
  transfers between devices with their start and end apart: 12, of which 3 were waited for; matrix products, arithmetic and copies ran while one was open for 8% of the time, Pallas kernels for 0%

commit v1 on v0

--- a/solution.py
+++ b/solution.py
@@ -1,14 +1,19 @@
+import functools
 import jax
 import jax.numpy as jnp
 import numpy as np
 from jax import lax
+from jax.experimental import pallas as pl
+from jax.experimental.pallas import tpu as pltpu
 from jax.sharding import PartitionSpec as P
 
 GRID_DN = 8
 
 
-SPANS = ((-1, 0, 1), (0, 1, 3), (1, 3, 4))
 GROUPS = ((0, 4, 0, 0), (4, 6, 1, 0), (6, 8, -1, 0), (8, 10, 0, 1), (10, 12, 0, -1))
+LEVELS = (-1, 0, 0, 1)
+LEAF = 8
+HIGH = lax.Precision.HIGHEST
 
 
 def shifted(value, axis, steps):
@@ -41,25 +46,235 @@
     return (upper >= 0) & (upper < count // GRID_DN) & (lower >= 0) & (lower < GRID_DN)
 
 
-def orthonormal(sketch):
-    gram = (
-        jnp.dot(
-            sketch.T, sketch, precision=lax.Precision.HIGHEST, preferred_element_type=jnp.float32
+def inverse_factor(gram, work, leaf):
+    size = gram.shape[0]
+    eye = (
+        lax.broadcasted_iota(jnp.int32, (size, size), 0)
+        == lax.broadcasted_iota(jnp.int32, (size, size), 1)
+    ).astype(jnp.float32)
+    trace = jnp.sum(jnp.sum(gram * eye, axis=0, keepdims=True), axis=1, keepdims=True)
+    ridge = 0.05 * trace / size + 1e-06
+    work[:, :size] = gram + ridge * eye
+    work[:, size:] = eye
+    for first in range(0, size, LEAF):
+        wide = []
+        for i in range(LEAF):
+            wide.append(work[first + i : first + i + 1, :])
+        entry = [
+            [
+                jnp.broadcast_to(wide[i][:, first + k : first + k + 1], (1, 2 * size))
+                for k in range(i + 1)
+            ]
+            for i in range(LEAF)
+        ]
+        for c in range(LEAF):
+            inverse = lax.rsqrt(entry[c][c])
+            wide[c] = wide[c] * inverse
+            scaled = [entry[i][c] * inverse if i > c else None for i in range(LEAF)]
+            for i in range(c + 1, LEAF):
+                for k in range(c + 1, i + 1):
+                    entry[i][k] = entry[i][k] - scaled[i] * scaled[k]
+                wide[i] = wide[i] - scaled[i] * wide[c]
+            leaf[c : c + 1, :] = wide[c]
+        rows = leaf[...]
+        if first + LEAF < size:
+            rest = first + LEAF
+            update = lax.dot_general(
+                rows[:, :size],
+                rows,
+                (((0,), (0,)), ((), ())),
+                precision=HIGH,
+                preferred_element_type=jnp.float32,
+            )
+            work[rest:, :] = work[rest:, :] - update[rest:, :]
+        work[first : first + LEAF, size:] = rows[:, size:]
+    return work[:, size:]
+
+
+def solve_kernel(
+    count,
+    theta,
+    omega,
+    left,
+    carry_out,
+    block,
+    sketch,
+    basis,
+    across,
+    projected,
+    work,
+    leaf,
+    norms,
+    norm_send,
+    norm_recv,
+    row_send,
+    row_recv,
+):
+    me = lax.axis_index("sec")
+    phys = theta.shape[0]
+    capacity = theta.shape[1]
+    rank = omega.shape[1]
+    width = theta.shape[2]
+    offsets = [(LEVELS[t // 4], LEVELS[t % 4]) for t in range(phys)]
+    barrier = pltpu.get_barrier_semaphore()
+
+    def greet(step, _):
+        pl.semaphore_signal(barrier, inc=1, device_id={"sec": lax.rem(me + step, count)})
+        return 0
+
+    lax.fori_loop(1, count, greet, 0)
+    pl.semaphore_wait(barrier, count - 1)
+
+    def rows_of(t):
+        return block.at[pl.ds(t * capacity, capacity)]
+
+    def remote(t):
+        up, down = offsets[t]
+        return pltpu.make_async_remote_copy(
+            src_ref=theta.at[t],
+            dst_ref=rows_of(t),
+            send_sem=row_send.at[t],
+            recv_sem=row_recv.at[t],
+            device_id={"sec": jnp.clip(me + up * GRID_DN + down, 0, count - 1)},
         )
-        / sketch.shape[0]
-    )
-    ridge = 0.05 * jnp.trace(gram) / gram.shape[0] + 1e-06
-    lower = jnp.linalg.cholesky(gram + ridge * jnp.eye(gram.shape[0], dtype=jnp.float32))
-    solved = jax.scipy.linalg.solve_triangular(lower, sketch.T, lower=True)
-    return solved.T.astype(jnp.bfloat16)
-
-
-def shifted_site(block, offset):
-    return shifted(block, "sec", offset)
-
-
-def moved_rows(block, offset):
-    return shifted(block, "sec", offset)
+
+    def local(t):
+        return pltpu.make_async_copy(theta.at[t], rows_of(t), row_recv.at[t])
+
+    order = sorted(range(phys), key=lambda t: (-abs(offsets[t][0]), -abs(offsets[t][1])))
+    for t in order:
+        up, down = offsets[t]
+        if up == 0 and down == 0:
+            local(t).start()
+        else:
+
+            @pl.when(inside(me, up, down, count))
+            def _(t=t):
+                remote(t).start()
+
+    for t in reversed(order):
+        up, down = offsets[t]
+        rows = pl.ds(t * capacity, capacity)
+        if up == 0 and down == 0:
+            local(t).wait()
+        else:
+            arrives = inside(me, -up, -down, count)
+
+            @pl.when(arrives)
+            def _(t=t):
+                remote(t).wait_recv()
+
+            @pl.when(jnp.logical_not(arrives))
+            def _(t=t, rows=rows):
+                block[rows, :] = jnp.zeros((capacity, width), block.dtype)
+
+        sketch[rows, :] = jnp.dot(
+            block[rows, :], omega[...], preferred_element_type=jnp.float32
+        )
+    for t in order:
+        up, down = offsets[t]
+        if up != 0 or down != 0:
+
+            @pl.when(inside(me, up, down, count))
+            def _(t=t):
+                remote(t).wait_send()
+
+    def orthonormal(out):
+        gram = lax.dot_general(
+            sketch[...],
+            sketch[...],
+            (((0,), (0,)), ((), ())),
+            precision=HIGH,
+            preferred_element_type=jnp.float32,
+        ) / (phys * capacity)
+        inverse = inverse_factor(gram, work, leaf)
+        out[...] = lax.dot_general(
+            sketch[...],
+            inverse,
+            (((1,), (1,)), ((), ())),
+            precision=HIGH,
+            preferred_element_type=jnp.float32,
+        ).astype(out.dtype)
+
+    def project(factor, out):
+        out[...] = lax.dot_general(
+            factor[...],
+            block[...],
+            (((0,), (0,)), ((), ())),
+            preferred_element_type=jnp.float32,
+        ).astype(out.dtype)
+
+    orthonormal(basis)
+    project(basis, across)
+    sketch[...] = lax.dot_general(
+        block[...], across[...], (((1,), (1,)), ((), ())), preferred_element_type=jnp.float32
+    )
+    orthonormal(basis)
+    left[...] = basis[...]
+    project(basis, projected)
+    squares = projected[...] * projected[...]
+    partial = jnp.sum(squares.reshape(rank // 8, 8, width), axis=0)
+    folded = partial[:, :128]
+    for first in range(128, width, 128):
+        folded = folded + partial[:, first : first + 128]
+    norms[me] = folded
+
+    def share(step):
+        return pltpu.make_async_remote_copy(
+            src_ref=norms.at[me],
+            dst_ref=norms.at[me],
+            send_sem=norm_send.at[step],
+            recv_sem=norm_recv.at[step],
+            device_id={"sec": lax.rem(me + step, count)},
+        )
+
+    def begin(step, _):
+        share(step).start()
+        return 0
+
+    def finish(step, _):
+        share(step).wait()
+        return 0
+
+    lax.fori_loop(1, count, begin, 0)
+    lax.fori_loop(1, count, finish, 0)
+    summed = jnp.sum(norms[...], axis=0)
+    total = jnp.sum(jnp.sum(summed, axis=0, keepdims=True), axis=1, keepdims=True)
+    carry_out[...] = (projected[...] * jnp.sqrt(count / total)).astype(carry_out.dtype)
+
+
+def solve(theta, omega, count):
+    phys, capacity, width = theta.shape
+    rank = omega.shape[1]
+    rows = phys * capacity
+    vmem = pl.BlockSpec(memory_space=pltpu.VMEM)
+    return pl.pallas_call(
+        functools.partial(solve_kernel, count),
+        out_shape=(
+            jax.ShapeDtypeStruct((rows, rank), jnp.bfloat16),
+            jax.ShapeDtypeStruct((rank, width), jnp.bfloat16),
+        ),
+        in_specs=[pl.BlockSpec(memory_space=pl.ANY), vmem],
+        out_specs=(vmem, vmem),
+        scratch_shapes=[
+            pltpu.VMEM((rows, width), jnp.bfloat16),
+            pltpu.VMEM((rows, rank), jnp.float32),
+            pltpu.VMEM((rows, rank), jnp.bfloat16),
+            pltpu.VMEM((rank, width), jnp.bfloat16),
+            pltpu.VMEM((rank, width), jnp.float32),
+            pltpu.VMEM((rank, 2 * rank), jnp.float32),
+            pltpu.VMEM((LEAF, 2 * rank), jnp.float32),
+            pltpu.VMEM((count, 8, 128), jnp.float32),
+            pltpu.SemaphoreType.DMA((count,)),
+            pltpu.SemaphoreType.DMA((count,)),
+            pltpu.SemaphoreType.DMA((phys,)),
+            pltpu.SemaphoreType.DMA((phys,)),
+        ],
+        compiler_params=pltpu.CompilerParams(
+            collective_id=0, has_side_effects=True, vmem_limit_bytes=40 * 1024 * 1024
+        ),
+        name="solve",
+    )(theta, omega)
 
 
 def body(carry, site, mpo, omega, sector_sizes):
@@ -86,7 +301,7 @@
     pieces = []
     for first_bond, last_bond, shift_up, shift_down in GROUPS:
         offset = shift_up * GRID_DN + shift_down
-        source = site_masked if offset == 0 else shifted_site(site_masked, offset)
+        source = site_masked if offset == 0 else shifted(site_masked, "sec", offset)
         valid = inside(sector, -shift_up, -shift_down, count)
         carry_part = carry_three[:, first_bond:last_bond]
         carry_part = jnp.where(valid, carry_part, jnp.zeros_like(carry_part))
@@ -107,31 +322,9 @@
         "awsb,wtsv->tavb", partial_sum, operator, preferred_element_type=jnp.float32
     )
     joined = jnp.where(target_ok[:, None, None, None], joined, 0.0).astype(jnp.bfloat16)
-    blocks = joined.reshape(4, 4, capacity, bond_width * capacity)
-    row_groups = []
-    for shift_up, up_first, up_last in SPANS:
-        pieces_row = []
-        for shift_down, down_first, down_last in SPANS:
-            part = blocks[up_first:up_last, down_first:down_last]
-            offset = shift_up * GRID_DN + shift_down
-            pieces_row.append(part if offset == 0 else moved_rows(part, offset))
-        row_groups.append(jnp.concatenate(pieces_row, 1))
-    gathered = jnp.concatenate(row_groups, 0)
-    block = gathered.reshape(phys_width * capacity, bond_width * capacity)
-    contract_rows = (((0,), (0,)), ((), ()))
-    first_sketch = jnp.dot(block, omega, preferred_element_type=jnp.float32)
-    basis = orthonormal(first_sketch)
-    across = lax.dot_general(
-        block, basis, contract_rows, preferred_element_type=jnp.float32
-    ).astype(jnp.bfloat16)
-    second_sketch = jnp.dot(block, across, preferred_element_type=jnp.float32)
-    left_basis = orthonormal(second_sketch)
-    projected = lax.dot_general(
-        left_basis, block, contract_rows, preferred_element_type=jnp.float32
-    )
-    total = lax.psum(jnp.sum(projected * projected), "sec")
-    next_carry = (projected * jnp.sqrt(count / total)).astype(jnp.bfloat16)
-    return (left_basis.reshape(1, phys_width, capacity, left_basis.shape[1]), next_carry[None])
+    theta = joined.reshape(phys_width, capacity, bond_width * capacity)
+    left, next_carry = solve(theta, omega, count)
+    return (left.reshape(1, phys_width, capacity, omega.shape[1]), next_carry[None])
 
 
 def solution(mesh):

time: 229 us -> 136 us (0.59)
  Pallas kernels: 0 us -> 71.6 us
  other arithmetic: 56.5 us -> 5.06 us
  starting transfers between devices: 49 us -> 10.7 us
  blocking collectives: 33.7 us -> 0 us
  matrix products: 32.7 us -> 10.3 us
  local copies, waits for them, and re-layouts: 40.9 us -> 29 us
  waiting for transfers between devices: 12.2 us -> 7.48 us
    pallas_call x0 -> x1, Pallas kernels: none -> 71.6 us  [solve(): pl.pallas_call(functools.partial(solve_kernel, count), out_shape=(jax.Sha...]
    another operation x10 -> x0, other arithmetic: 45.7 us -> none  [the longest x6 24.8 us: orthonormal(): jnp.linalg.cholesky(gram + ridge * jnp.eye(gram.shape[0], dtype=jnp.float...]
    ppermute x12 -> x4, starting transfers between devices: 49 us -> 10.7 us  [shifted(): lax.ppermute(value, axis, [(source, source + steps) for source in range(i...]
    psum x1 -> x0, blocking collectives: 33.7 us -> none  [body(): total = lax.psum(jnp.sum(projected * projected), 'sec')]
    dot_general x5 -> x0, matrix products: 17.4 us -> none  [the longest x1 6.8 us: body(): second_sketch = jnp.dot(block, across, preferred_element_type=jnp.float32)]
    slice x8 -> x0, local copies, waits for them, and re-layouts: 8.85 us -> none  [body(): part = blocks[up_first:up_last, down_first:down_last]]
    concatenate x1 -> x0, local copies, waits for them, and re-layouts: 6.46 us -> none  [body(): gathered = jnp.concatenate(row_groups, 0)]
    reshape x0 -> x1, local copies, waits for them, and re-layouts: none -> 4.89 us  [body(): theta = joined.reshape(phys_width, capacity, bond_width * capacity)]
  transfers between devices with their start and end apart: 12 -> 4, of which waited for: 3 -> 1; matrix products, arithmetic and copies ran while one was open for 8% -> 7% of each run, Pallas kernels for 0% -> 0%
where the time goes in v1:
time: 136 us; the launch traced here: 135 us
  Pallas kernels  71.6 us (53%)
  local copies, waits for them, and re-layouts  29 us (21%)
  starting transfers between devices  10.7 us (8%)
  matrix products  10.3 us (8%)
  waiting for transfers between devices  7.48 us (6%)
  other arithmetic  5.06 us (4%)
    pallas_call x1, Pallas kernels, solve(): pl.pallas_call(functools.partial(solve_kernel, count), out_shape=(jax.Sha...  71.6 us
    ppermute x4, starting transfers between devices, shifted(): lax.ppermute(value, axis, [(source, source + steps) for source in range(i...  10.7 us
    unnamed x13, local copies, waits for them, and re-layouts  8.63 us
    ppermute x4, waiting for transfers between devices, shifted(): lax.ppermute(value, axis, [(source, source + steps) for source in range(i...  7.48 us
    convert_element_type x1, local copies, waits for them, and re-layouts, body(): jnp.where(target_ok[:, None, None, None], joined, 0.0).astype(jnp.bfloat16)  7.09 us
    dot_general x1, matrix products, body(): jnp.einsum('awsb,wtsv->tavb', partial_sum, operator, preferred_element_ty...  6.73 us
    reshape x1, local copies, waits for them, and re-layouts, body(): theta = joined.reshape(phys_width, capacity, bond_width * capacity)  4.89 us
    concatenate x5, local copies, waits for them, and re-layouts, body(): jnp.concatenate(pieces, 1).astype(jnp.bfloat16)  4.87 us
  transfers between devices with their start and end apart: 4, of which 1 were waited for; matrix products, arithmetic and copies ran while one was open for 7% of the time, Pallas kernels for 0%

profile of v1, /device:TPU:0, one launch (start us, length us, event | category | flops | bytes accessed | tf_op | source)
XLA Modules:
  0.0 134.9 jit_solution(9198810408123693994)
XLA Ops:
  2.2 1.3 gather_fusion
  3.8 1.2 dynamic_slice.3
  5.7 1.8 %and_select_fusion = bf16[96,1536]{1,0:T(8,128)(2,1)} fusion(bf16[1,96,1536]{2,1,0:T(8,128)(2,1)} %param.10, pred[1536]{0:T(1024)(128)(4,1)S(1)} %compare_and_fusion, pred[96]{0:T(512)(128)(4,1)S(1)} %iota_compare_fusion), kind=kLoop, calls=%fused_computation.18 | loop fusion | flops 294912 | bytes 591456 | tf_op jit(solution)/shard_map/jit(_where)/select_n | solution.py:294
  7.5 6.0 %collective-permute-start = (bf16[96,1536]{1,0:T(8,128)(2,1)}, bf16[96,1536]{1,0:T(8,128)(2,1)S(1)}, u32[]{:S(2)}, u32[]{:S(2)}) collective-permute-start(bf16[96,1536]{1,0:T(8,128)(2,1)} %and_select_fusion), channel_id=1, source_target_pairs={{0,8},{1,9},{2,10},{3,11},{4,12},{5,13},{6,14},{7,15},{16,24},{17,... | collective-permute-start | bytes 884744 | tf_op jit(solution)/shard_map/ppermute | solution.py:22
  13.5 1.3 collective-permute-start.1
  14.8 2.2 %collective-permute-start.2 = (bf16[96,1536]{1,0:T(8,128)(2,1)}, bf16[96,1536]{1,0:T(8,128)(2,1)}, u32[]{:S(2)}, u32[]{:S(2)}) collective-permute-start(bf16[96,1536]{1,0:T(8,128)(2,1)} %and_select_fusion), channel_id=1, source_target_pairs={{0,1},{1,2},{2,3},{3,4},{4,5},{5,6},{6,7},{7,8},{8,9},{9,10},{10,1... | collective-permute-start | bytes 884744 | tf_op jit(solution)/shard_map/ppermute | solution.py:22
  17.0 1.3 collective-permute-start.3
  18.3 1.1 fusion.10
  19.7 1.1 copy.17
  21.8 1.8 %fusion.6 = bf16[96,12,16,96]{3,2,1,0:T(8,128)(2,1)} fusion(bf16[96,4,16,96]{3,0,2,1:T(8,128)(2,1)S(1)} %fusion.8), kind=kLoop, calls=%fused_computation.11 | loop fusion | bytes 2752512
  23.9 7.5 %collective-permute-done.1 = bf16[96,1536]{1,0:T(8,128)(2,1)S(1)} collective-permute-done((bf16[96,1536]{1,0:T(8,128)(2,1)}, bf16[96,1536]{1,0:T(8,128)(2,1)S(1)}, u32[]{:S(2)}, u32[]{:S(2)}) %collective-permute-start.1) | collective-permute-done | bytes 294944 | tf_op jit(solution)/shard_map/ppermute | solution.py:22
  33.0 1.3 convolution_convert_fusion.1
  34.9 1.1 convolution_convert_fusion
  36.1 1.8 %concatenate.16 = bf16[96,2,16,96]{3,2,0,1:T(8,128)(2,1)S(1)} reshape(bf16[96,2,1536]{2,0,1:T(8,128)(2,1)} %convolution_convert_fusion) | data formatting | bytes 1179648 | tf_op jit(solution)/shard_map/concatenate | solution.py:316
  37.9 1.1 copy_dynamic-update-slice_fusion.3
  39.0 1.1 copy_dynamic-update-slice_fusion.2
  40.1 1.0 copy_dynamic-update-slice_fusion.1
  41.1 1.1 copy_dynamic-update-slice_fusion
  42.2 6.7 %fusion.1 = bf16[16,96,12,96]{3,0,1,2:T(8,128)(2,1)} fusion(pred[16]{0:T(512)(128)(4,1)S(1)} %compare_and_fusion.1, bf16[96,12,16,96]{3,2,1,0:T(8,128)(2,1)} %copy_dynamic-update-slice_fusion, pred[12,16,16,12]{2,1,3,0:T(8,128)(4,1)S(1)} %copy-done.2, bf16[12,16,16,12]{2,1,3,0:T(8,128)(2,1)S(1)} %copy-done.1), kind=kOutput, calls=%fused_computation.3 | convolution fusion | flops 683053056 | bytes 7188496 | tf_op jit(solution)/shard_map/awsb,wtsv->tavb/dot_general | solution.py:321
  49.0 7.1 %copy.24 = bf16[16,96,12,96]{1,3,2,0:T(8,128)(2,1)} copy(bf16[16,96,12,96]{3,0,1,2:T(8,128)(2,1)} %fusion.1) | data formatting | bytes 7077888 | tf_op jit(solution)/shard_map/convert_element_type | solution.py:324
  56.1 4.9 %copy.25.theta = bf16[16,96,1152]{2,1,0:T(8,128)(2,1)S(1)} copy(bf16[16,96,1152]{1,2,0:T(8,128)(2,1)} %bitcast.60) | data formatting | bytes 7077888 | tf_op jit(solution)/shard_map/reshape | solution.py:325
  61.0 1.0 copy-done
  61.9 71.6 %solve.1 = (bf16[1536,128]{1,0:T(8,128)(2,1)S(1)}, bf16[128,1152]{1,0:T(8,128)(2,1)S(1)}) custom-call(bf16[16,96,1152]{2,1,0:T(8,128)(2,1)S(1)} %copy.25.theta, bf16[1152,128]{1,0:T(8,128)(2,1)S(1)} %copy-done), custom_call_target="tpu_custom_call" | custom-call | tf_op jit(solution)/shard_map/solve/pallas_call | solution.py:251
  133.5 0.7 copy.50
  (29 shorter events, 6.9 us)
Async XLA Ops:
  7.5 16.1 %collective-permute-start = (bf16[96,1536]{1,0:T(8,128)(2,1)}, bf16[96,1536]{1,0:T(8,128)(2,1)S(1)}, u32[]{:S(2)}, u32[]{:S(2)}) collective-permute-start(bf16[96,1536]{1,0:T(8,128)(2,1)} %and_select_fusion), channel_id=1, source_target_pairs={{0,8},{1,9},{2,10},{3,11},{4,12},{5,13},{6,14},{7,15},{16,24},{17,... | collective-permute-start | bytes 884744 | tf_op jit(solution)/shard_map/ppermute | solution.py:22
  13.5 17.9 %collective-permute-start.1 = (bf16[96,1536]{1,0:T(8,128)(2,1)}, bf16[96,1536]{1,0:T(8,128)(2,1)S(1)}, u32[]{:S(2)}, u32[]{:S(2)}) collective-permute-start(bf16[96,1536]{1,0:T(8,128)(2,1)} %and_select_fusion), channel_id=1, source_target_pairs={{8,0},{9,1},{10,2},{11,3},{12,4},{13,5},{14,6},{15,7},{24,16},{25,... | collective-permute-start | bytes 884744 | tf_op jit(solution)/shard_map/ppermute | solution.py:22
  14.8 18.2 %collective-permute-start.2 = (bf16[96,1536]{1,0:T(8,128)(2,1)}, bf16[96,1536]{1,0:T(8,128)(2,1)}, u32[]{:S(2)}, u32[]{:S(2)}) collective-permute-start(bf16[96,1536]{1,0:T(8,128)(2,1)} %and_select_fusion), channel_id=1, source_target_pairs={{0,1},{1,2},{2,3},{3,4},{4,5},{5,6},{6,7},{7,8},{8,9},{9,10},{10,1... | collective-permute-start | bytes 884744 | tf_op jit(solution)/shard_map/ppermute | solution.py:22
  17.0 18.0 %collective-permute-start.3 = (bf16[96,1536]{1,0:T(8,128)(2,1)}, bf16[96,1536]{1,0:T(8,128)(2,1)S(1)}, u32[]{:S(2)}, u32[]{:S(2)}) collective-permute-start(bf16[96,1536]{1,0:T(8,128)(2,1)} %and_select_fusion), channel_id=1, source_target_pairs={{1,0},{2,1},{3,2},{4,3},{5,4},{6,5},{7,6},{8,7},{9,8},{10,9},{11,1... | collective-permute-start | bytes 884744 | tf_op jit(solution)/shard_map/ppermute | solution.py:22
  36.1 6.1 %copy-start.2 = (pred[12,16,16,12]{2,1,3,0:T(8,128)(4,1)S(1)}, pred[12,16,16,12]{2,1,3,0:T(8,128)(4,1)}, u32[]{:S(2)}) copy-start(pred[12,16,16,12]{2,1,3,0:T(8,128)(4,1)} %constant.82.clone) | copy-start | bytes 110596
  37.9 4.3 %copy-start.1 = (bf16[12,16,16,12]{2,1,3,0:T(8,128)(2,1)S(1)}, bf16[12,16,16,12]{2,1,3,0:T(8,128)(2,1)}, u32[]{:S(2)}) copy-start(bf16[12,16,16,12]{2,1,3,0:T(8,128)(2,1)} %param.11) | copy-start | bytes 221188
  60.9 1.0 copy-start

commit v2 on v1

--- a/solution.py
+++ b/solution.py
@@ -277,52 +277,112 @@
     )(theta, omega)
 
 
+def theta_kernel(carry, matrix, live, own, *rest):
+    sites = (own,) + rest[:4]
+    theta, parts, rows = rest[4:]
+    width, capacity = carry.shape[0], carry.shape[1]
+    phys = theta.shape[0]
+    pairs = width * phys
+    pad = jnp.zeros((capacity, 128 - capacity % 128), own.dtype)
+    for s in range(phys):
+        for (first, last, _, _), source in zip(GROUPS, sites):
+            piece = jnp.concatenate([source[:, s * capacity : (s + 1) * capacity], pad], 1)
+            product = jnp.dot(
+                carry[first:last].reshape((last - first) * capacity, capacity),
+                piece,
+                preferred_element_type=jnp.float32,
+            )
+            for w in range(first, last):
+                at = (w - first) * capacity
+                parts[pl.ds(w * phys + s, capacity, stride=PITCH), :] = product[at : at + capacity]
+
+    def apply(step, _):
+        for inner in range(0, UNROLL, 2):
+            a = step * UNROLL + inner
+            pair = [
+                parts[pl.ds(pl.multiple_of((a + k) * PITCH, 8), pairs), :].astype(jnp.bfloat16)
+                for k in range(2)
+            ]
+            out = jnp.dot(
+                matrix[...], jnp.concatenate(pair, 1), preferred_element_type=jnp.float32
+            )
+            for k in range(2):
+                for v in range(width):
+                    rows[pl.ds(v * phys * capacity + a + k, phys, stride=capacity), :] = out[
+                        v * phys : (v + 1) * phys, k * 128 : (k + 1) * 128
+                    ]
+        return 0
+
+    lax.fori_loop(0, capacity // UNROLL, apply, 0)
+
+    def finish(t, _):
+        pieces = [
+            rows[pl.ds(pl.multiple_of((v * phys + t) * capacity, 8), capacity), :][:, :capacity]
+            for v in range(width)
+        ]
+        joined = jnp.concatenate(pieces, 1)
+        theta[t] = jnp.where(live[t] > 0.5, joined, 0.0).astype(theta.dtype)
+        return 0
+
+    lax.fori_loop(0, phys, finish, 0)
+
+
+PITCH = 200
+UNROLL = 8
+
+
+def make_theta(carry, matrix, live, sites):
+    width, capacity = carry.shape[0], carry.shape[1]
+    phys = live.shape[0]
+    vmem = pl.BlockSpec(memory_space=pltpu.VMEM)
+    return pl.pallas_call(
+        theta_kernel,
+        out_shape=jax.ShapeDtypeStruct((phys, capacity, width * capacity), jnp.bfloat16),
+        in_specs=[vmem] * (3 + len(sites)),
+        out_specs=vmem,
+        scratch_shapes=[
+            pltpu.VMEM((PITCH * capacity, 128), jnp.float32),
+            pltpu.VMEM((width * phys * capacity, 128), jnp.float32),
+        ],
+        compiler_params=pltpu.CompilerParams(vmem_limit_bytes=48 * 1024 * 1024),
+        name="theta",
+    )(carry, matrix, live, *sites)
+
+
 def body(carry, site, mpo, omega, sector_sizes):
     count = lax.axis_size("sec")
     sector = lax.axis_index("sec")
     capacity = carry.shape[1]
     bond_width = mpo.shape[0]
     phys_width = mpo.shape[1]
+    raw = site[0]
+    sites = [raw] + [shifted(raw, "sec", up * GRID_DN + down) for _, _, up, down in GROUPS[1:]]
     phys_up, phys_down, bond_up, bond_down = charge_tables()
     rows = jnp.arange(capacity, dtype=jnp.int32)
-    own_live = rows < sector_sizes[sector]
-    targets = sector + jnp.asarray(phys_up * GRID_DN + phys_down)
+
+    def sizes_at(up, down):
+        at = jnp.clip(sector + jnp.asarray(up * GRID_DN + down), 0, count - 1)
+        hit = at[..., None] == jnp.arange(count, dtype=jnp.int32)
+        found = jnp.sum(jnp.where(hit, sector_sizes, 0), -1)
+        return jnp.where(inside(sector, up, down, count), found, 0)
+
+    own_size = sizes_at(np.zeros((1,), np.int32), np.zeros((1,), np.int32))
+    source_sizes = sizes_at(-bond_up, -bond_down)
+    carry_live = (rows[None, :, None] < own_size) & (
+        rows[None, None, :] < source_sizes[:, None, None]
+    )
+    carry_three = carry[0].reshape(capacity, bond_width, capacity).transpose(1, 0, 2)
+    carry_three = jnp.where(carry_live, carry_three, jnp.zeros_like(carry_three))
+    column_sizes = sizes_at(
+        phys_up[:, None] - bond_up[None, :], phys_down[:, None] - bond_down[None, :]
+    )
     target_ok = inside(sector, phys_up, phys_down, count)
-    target_sizes = sector_sizes[jnp.clip(targets, 0, count - 1)]
-    column_live = target_ok[:, None] & (rows[None, :] < target_sizes[:, None])
-    site_four = site[0].reshape(capacity, phys_width, capacity)
-    site_masked = jnp.where(
-        own_live[:, None, None] & column_live[None, :, :], site_four, jnp.zeros_like(site_four)
-    )
-    site_masked = site_masked.reshape(capacity, phys_width * capacity)
-    carry_three = jnp.where(own_live[:, None], carry[0], jnp.zeros_like(carry[0])).reshape(
-        capacity, bond_width, capacity
-    )
-    pieces = []
-    for first_bond, last_bond, shift_up, shift_down in GROUPS:
-        offset = shift_up * GRID_DN + shift_down
-        source = site_masked if offset == 0 else shifted(site_masked, "sec", offset)
-        valid = inside(sector, -shift_up, -shift_down, count)
-        carry_part = carry_three[:, first_bond:last_bond]
-        carry_part = jnp.where(valid, carry_part, jnp.zeros_like(carry_part))
-        group_width = last_bond - first_bond
-        product = jnp.dot(
-            carry_part.reshape(capacity * group_width, capacity),
-            source,
-            preferred_element_type=jnp.float32,
-        )
-        pieces.append(product.reshape(capacity, group_width, phys_width * capacity))
-    partial_sum = (
-        jnp.concatenate(pieces, 1)
-        .astype(jnp.bfloat16)
-        .reshape(capacity, bond_width, phys_width, capacity)
-    )
+    live = (rows[None, None, :] < column_sizes[:, :, None]) & target_ok[:, None, None]
+    live = live.astype(jnp.float32).reshape(phys_width, 1, bond_width * capacity)
     operator = jnp.where(jnp.asarray(conserving()), mpo, jnp.zeros_like(mpo))
-    joined = jnp.einsum(
-        "awsb,wtsv->tavb", partial_sum, operator, preferred_element_type=jnp.float32
-    )
-    joined = jnp.where(target_ok[:, None, None, None], joined, 0.0).astype(jnp.bfloat16)
-    theta = joined.reshape(phys_width, capacity, bond_width * capacity)
+    pairs = phys_width * bond_width
+    matrix = operator.transpose(3, 1, 0, 2).reshape(pairs, pairs)
+    theta = make_theta(carry_three, matrix, live, sites)
     left, next_carry = solve(theta, omega, count)
     return (left.reshape(1, phys_width, capacity, omega.shape[1]), next_carry[None])
 

time: 136 us -> 116 us (0.85)
  local copies, waits for them, and re-layouts: 29 us -> 4.23 us
  Pallas kernels: 71.6 us -> 90 us
  matrix products: 10.3 us -> 0 us
  waiting for transfers between devices: 7.48 us -> 0.01 us
  other arithmetic: 5.06 us -> 8.17 us
  starting transfers between devices: 10.7 us -> 12.1 us
    pallas_call x0 -> x1, Pallas kernels: none -> 12.7 us  [make_theta(): pl.pallas_call(theta_kernel, out_shape=jax.ShapeDtypeStruct((phys, capaci...]
    dot_general x6 -> x0, matrix products: 10.3 us -> none  [the longest x1 6.73 us: body(): jnp.einsum('awsb,wtsv->tavb', partial_sum, operator, preferred_element_ty...]
    ppermute x4, waiting for transfers between devices: 7.48 us -> 0.01 us  [shifted(): lax.ppermute(value, axis, [(source, source + steps) for source in range(i...]
    convert_element_type x1 -> x0, local copies, waits for them, and re-layouts: 7.09 us -> none  [body(): jnp.where(target_ok[:, None, None, None], joined, 0.0).astype(jnp.bfloat16)]
    unnamed x13 -> x7, local copies, waits for them, and re-layouts: 8.63 us -> 2.62 us
    pallas_call x1, Pallas kernels: 71.6 us -> 77.3 us  [solve(): pl.pallas_call(functools.partial(solve_kernel, count), out_shape=(jax.Sha...]
    concatenate x5 -> x0, local copies, waits for them, and re-layouts: 4.87 us -> none  [body(): jnp.concatenate(pieces, 1).astype(jnp.bfloat16)]
    reshape x1, local copies, waits for them, and re-layouts: 4.89 us -> 0.61 us  [body(): matrix = operator.transpose(3, 1, 0, 2).reshape(pairs, pairs)]
  transfers between devices with their start and end apart: 4 -> 4, of which waited for: 1 -> 0; matrix products, arithmetic and copies ran while one was open for 7% -> 9% of each run, Pallas kernels for 0% -> 0%
where the time goes in v2:
time: 116 us
  Pallas kernels  90 us (78%)
  starting transfers between devices  12.1 us (10%)
  other arithmetic  8.17 us (7%)
  local copies, waits for them, and re-layouts  4.23 us (4%)
  between operations  1.49 us (1%)
    pallas_call x1, Pallas kernels, solve(): pl.pallas_call(functools.partial(solve_kernel, count), out_shape=(jax.Sha...  77.3 us
    pallas_call x1, Pallas kernels, make_theta(): pl.pallas_call(theta_kernel, out_shape=jax.ShapeDtypeStruct((phys, capaci...  12.7 us
    ppermute x4, starting transfers between devices, shifted(): lax.ppermute(value, axis, [(source, source + steps) for source in range(i...  12.1 us
    reduce_sum x3, other arithmetic, sizes_at(): found = jnp.sum(jnp.where(hit, sector_sizes, 0), -1)  3.13 us
    unnamed x7, local copies, waits for them, and re-layouts  2.62 us
  transfers between devices with their start and end apart: 4, of which 0 were waited for; matrix products, arithmetic and copies ran while one was open for 9% of the time, Pallas kernels for 0%

profile of v2, /device:TPU:0, one launch (start us, length us, event | category | flops | bytes accessed | tf_op | source)
XLA Modules:
  0.0 116.0 jit_solution(9999558238957273213)
XLA Ops:
  0.6 1.4 %collective-permute-start.3 = (bf16[96,1536]{1,0:T(8,128)(2,1)}, bf16[96,1536]{1,0:T(8,128)(2,1)S(1)}, u32[]{:S(2)}, u32[]{:S(2)}) collective-permute-start(bf16[96,1536]{1,0:T(8,128)(2,1)} %bitcast.10), channel_id=1, source_target_pairs={{1,0},{2,1},{3,2},{4,3},{5,4},{6,5},{7,6},{8,7},{9,8},{10,9},{11,1... | collective-permute-start | bytes 884744 | tf_op jit(solution)/shard_map/ppermute | solution.py:22
  2.1 3.0 %collective-permute-start.2 = (bf16[96,1536]{1,0:T(8,128)(2,1)}, bf16[96,1536]{1,0:T(8,128)(2,1)S(1)}, u32[]{:S(2)}, u32[]{:S(2)}) collective-permute-start(bf16[96,1536]{1,0:T(8,128)(2,1)} %bitcast.11), channel_id=1, source_target_pairs={{0,1},{1,2},{2,3},{3,4},{4,5},{5,6},{6,7},{7,8},{8,9},{9,10},{10,1... | collective-permute-start | bytes 884744 | tf_op jit(solution)/shard_map/ppermute | solution.py:22
  5.1 1.3 %collective-permute-start.1 = (bf16[96,1536]{1,0:T(8,128)(2,1)}, bf16[96,1536]{1,0:T(8,128)(2,1)S(1)}, u32[]{:S(2)}, u32[]{:S(2)}) collective-permute-start(bf16[96,1536]{1,0:T(8,128)(2,1)} %bitcast.12), channel_id=1, source_target_pairs={{8,0},{9,1},{10,2},{11,3},{12,4},{13,5},{14,6},{15,7},{24,16},{25,... | collective-permute-start | bytes 884744 | tf_op jit(solution)/shard_map/ppermute | solution.py:22
  6.4 6.3 %collective-permute-start = (bf16[96,1536]{1,0:T(8,128)(2,1)}, bf16[96,1536]{1,0:T(8,128)(2,1)S(1)}, u32[]{:S(2)}, u32[]{:S(2)}) collective-permute-start(bf16[96,1536]{1,0:T(8,128)(2,1)} %bitcast.13), channel_id=1, source_target_pairs={{0,8},{1,9},{2,10},{3,11},{4,12},{5,13},{6,14},{7,15},{16,24},{17,... | collective-permute-start | bytes 884744 | tf_op jit(solution)/shard_map/ppermute | solution.py:22
  12.8 0.7 add_clamp_fusion.1
  13.4 1.3 %fusion.4 = s32[]{:T(128)} fusion(s32[16]{0:T(128)} %param.21, s32[]{:T(128)S(6)} %min.27), kind=kLoop, calls=%fused_computation.20 | loop fusion | flops 47 | bytes 72 | tf_op jit(solution)/shard_map/reduce_sum | solution.py:366
  14.7 0.8 select_reduce_fusion.1
  15.6 0.7 and_select_fusion.1
  16.3 0.7 add_clamp_fusion
  17.0 1.0 select_reduce_fusion
  18.0 0.7 fusion.3
  19.0 0.2 lt.126
  19.9 0.7 compare_and_fusion
  20.5 1.2 %select_bitcast_fusion = bf16[12,16,12,16]{3,1,0,2:T(8,128)(2,1)S(1)} fusion(pred[12,16,16,12]{2,1,3,0:T(8,128)(4,1)} %constant.96.clone, bf16[12,16,16,12]{2,1,3,0:T(8,128)(2,1)} %param.19), kind=kLoop, calls=%fused_computation | loop fusion | flops 36864 | bytes 184320 | tf_op jit(solution)/shard_map/transpose | solution.py:384
  21.8 0.1 and_convert_fusion.live
  21.9 1.1 copy.29
  23.0 0.2 copy.30
  23.2 0.4 copy.31
  23.7 0.6 reshape.103.matrix
  24.3 0.2 and_select_fusion.carry
  24.5 12.7 %theta.1 = bf16[16,96,1152]{2,1,0:T(8,128)(2,1)S(1)} custom-call(bf16[12,96,96]{2,1,0:T(8,128)(2,1)S(1)} %and_select_fusion.carry, bf16[192,192]{1,0:T(8,128)(2,1)S(1)} %reshape.103.matrix, f32[16,1,1152]{2,1,0:T(1,128)S(1)} %and_convert_fusion.live, bf16[96,1536]{1,0:T(8,128)(2,1)S(1)} %bitcast.14, bf16[96,1536]{1,0:T(8,128)(2,1)S(1)} %collective-permute-done.rest_0_, ...), custom_call_target="tpu_custom_call" | custom-call | tf_op jit(solution)/shard_map/theta/pallas_call | solution.py:338
  37.2 77.3 %solve.1 = (bf16[1536,128]{1,0:T(8,128)(2,1)S(1)}, bf16[128,1152]{1,0:T(8,128)(2,1)S(1)}) custom-call(bf16[16,96,1152]{2,1,0:T(8,128)(2,1)S(1)} %theta.1, bf16[1152,128]{1,0:T(8,128)(2,1)S(1)} %copy-done.1), custom_call_target="tpu_custom_call" | custom-call | tf_op jit(solution)/shard_map/solve/pallas_call | solution.py:251
  114.5 0.7 copy.37
  115.2 0.7 copy.38
  (14 shorter events, 0.4 us)
Async XLA Ops:
  0.6 23.9 %copy-start = (bf16[1,96,1536]{2,1,0:T(8,128)(2,1)S(1)}, bf16[1,96,1536]{2,1,0:T(8,128)(2,1)}, u32[]{:S(2)}) copy-start(bf16[1,96,1536]{2,1,0:T(8,128)(2,1)} %param.18) | copy-start | bytes 884740
  0.6 23.8 %collective-permute-start.3 = (bf16[96,1536]{1,0:T(8,128)(2,1)}, bf16[96,1536]{1,0:T(8,128)(2,1)S(1)}, u32[]{:S(2)}, u32[]{:S(2)}) collective-permute-start(bf16[96,1536]{1,0:T(8,128)(2,1)} %bitcast.10), channel_id=1, source_target_pairs={{1,0},{2,1},{3,2},{4,3},{5,4},{6,5},{7,6},{8,7},{9,8},{10,9},{11,1... | collective-permute-start | bytes 884744 | tf_op jit(solution)/shard_map/ppermute | solution.py:22
  2.1 22.4 %collective-permute-start.2 = (bf16[96,1536]{1,0:T(8,128)(2,1)}, bf16[96,1536]{1,0:T(8,128)(2,1)S(1)}, u32[]{:S(2)}, u32[]{:S(2)}) collective-permute-start(bf16[96,1536]{1,0:T(8,128)(2,1)} %bitcast.11), channel_id=1, source_target_pairs={{0,1},{1,2},{2,3},{3,4},{4,5},{5,6},{6,7},{7,8},{8,9},{9,10},{10,1... | collective-permute-start | bytes 884744 | tf_op jit(solution)/shard_map/ppermute | solution.py:22
  5.1 19.3 %collective-permute-start.1 = (bf16[96,1536]{1,0:T(8,128)(2,1)}, bf16[96,1536]{1,0:T(8,128)(2,1)S(1)}, u32[]{:S(2)}, u32[]{:S(2)}) collective-permute-start(bf16[96,1536]{1,0:T(8,128)(2,1)} %bitcast.12), channel_id=1, source_target_pairs={{8,0},{9,1},{10,2},{11,3},{12,4},{13,5},{14,6},{15,7},{24,16},{25,... | collective-permute-start | bytes 884744 | tf_op jit(solution)/shard_map/ppermute | solution.py:22
  6.4 18.0 %collective-permute-start = (bf16[96,1536]{1,0:T(8,128)(2,1)}, bf16[96,1536]{1,0:T(8,128)(2,1)S(1)}, u32[]{:S(2)}, u32[]{:S(2)}) collective-permute-start(bf16[96,1536]{1,0:T(8,128)(2,1)} %bitcast.13), channel_id=1, source_target_pairs={{0,8},{1,9},{2,10},{3,11},{4,12},{5,13},{6,14},{7,15},{16,24},{17,... | collective-permute-start | bytes 884744 | tf_op jit(solution)/shard_map/ppermute | solution.py:22
  23.6 13.5 %copy-start.1 = (bf16[1152,128]{1,0:T(8,128)(2,1)S(1)}, bf16[1152,128]{1,0:T(8,128)(2,1)}, u32[]{:S(2)}) copy-start(bf16[1152,128]{1,0:T(8,128)(2,1)} %omega.1) | copy-start | bytes 884740

commit v3 on v2

--- a/solution.py
+++ b/solution.py
@@ -91,31 +91,39 @@
     return work[:, size:]
 
 
-def solve_kernel(
-    count,
-    theta,
-    omega,
-    left,
-    carry_out,
-    block,
-    sketch,
-    basis,
-    across,
-    projected,
-    work,
-    leaf,
-    norms,
-    norm_send,
-    norm_recv,
-    row_send,
-    row_recv,
-):
+def solve_kernel(count, paired, n_theta, *refs):
+    thetas, omega = refs[:n_theta], refs[n_theta]
+    (
+        left,
+        carry_out,
+        block,
+        sketch,
+        basis,
+        across,
+        projected,
+        work,
+        leaf,
+        norms,
+        norm_send,
+        norm_recv,
+        row_send,
+        row_recv,
+    ) = refs[n_theta + 1 :]
     me = lax.axis_index("sec")
-    phys = theta.shape[0]
-    capacity = theta.shape[1]
+    capacity = thetas[0].shape[1]
+    phys = block.shape[0] // capacity
     rank = omega.shape[1]
-    width = theta.shape[2]
-    offsets = [(LEVELS[t // 4], LEVELS[t % 4]) for t in range(phys)]
+    width = block.shape[1]
+    if paired:
+        inner, swapped = thetas
+        crossing = swapped.shape[0]
+        entry_row = (me // GRID_DN) * (phys - crossing)
+        items = [(swapped.at[k], entry_row + k, 0, LEVELS[k]) for k in range(crossing)] + [
+            (inner.at[k], crossing + k, 0, LEVELS[(crossing + k) % 4])
+            for k in range(inner.shape[0])
+        ]
+    else:
+        items = [(thetas[0].at[t], t, LEVELS[t // 4], LEVELS[t % 4]) for t in range(phys)]
     barrier = pltpu.get_barrier_semaphore()
 
     def greet(step, _):
@@ -125,59 +133,66 @@
     lax.fori_loop(1, count, greet, 0)
     pl.semaphore_wait(barrier, count - 1)
 
-    def rows_of(t):
-        return block.at[pl.ds(t * capacity, capacity)]
-
-    def remote(t):
-        up, down = offsets[t]
+    def rows_of(n):
+        start = items[n][1] * capacity
+        return pl.ds(start if isinstance(start, int) else pl.multiple_of(start, 16), capacity)
+
+    def remote(n):
+        source, _, up, down = items[n]
         return pltpu.make_async_remote_copy(
-            src_ref=theta.at[t],
-            dst_ref=rows_of(t),
-            send_sem=row_send.at[t],
-            recv_sem=row_recv.at[t],
+            src_ref=source,
+            dst_ref=block.at[rows_of(n)],
+            send_sem=row_send.at[n],
+            recv_sem=row_recv.at[n],
             device_id={"sec": jnp.clip(me + up * GRID_DN + down, 0, count - 1)},
         )
 
-    def local(t):
-        return pltpu.make_async_copy(theta.at[t], rows_of(t), row_recv.at[t])
-
-    order = sorted(range(phys), key=lambda t: (-abs(offsets[t][0]), -abs(offsets[t][1])))
-    for t in order:
-        up, down = offsets[t]
+    def local(n):
+        return pltpu.make_async_copy(items[n][0], block.at[rows_of(n)], row_recv.at[n])
+
+    order = sorted(range(len(items)), key=lambda n: (-abs(items[n][2]), -abs(items[n][3])))
+    for n in order:
+        _, _, up, down = items[n]
         if up == 0 and down == 0:
-            local(t).start()
+            local(n).start()
         else:
 
             @pl.when(inside(me, up, down, count))
-            def _(t=t):
-                remote(t).start()
-
-    for t in reversed(order):
-        up, down = offsets[t]
-        rows = pl.ds(t * capacity, capacity)
+            def _(n=n):
+                remote(n).start()
+
+    if paired:
+        empty = pl.ds(
+            pl.multiple_of((phys - crossing - entry_row) * capacity, 16), crossing * capacity
+        )
+        block[empty, :] = jnp.zeros((crossing * capacity, width), block.dtype)
+        sketch[empty, :] = jnp.zeros((crossing * capacity, rank), sketch.dtype)
+    for n in reversed(order):
+        _, _, up, down = items[n]
+        rows = rows_of(n)
         if up == 0 and down == 0:
-            local(t).wait()
+            local(n).wait()
         else:
             arrives = inside(me, -up, -down, count)
 
             @pl.when(arrives)
-            def _(t=t):
-                remote(t).wait_recv()
+            def _(n=n):
+                remote(n).wait_recv()
 
             @pl.when(jnp.logical_not(arrives))
-            def _(t=t, rows=rows):
+            def _(rows=rows):
                 block[rows, :] = jnp.zeros((capacity, width), block.dtype)
 
         sketch[rows, :] = jnp.dot(
             block[rows, :], omega[...], preferred_element_type=jnp.float32
         )
-    for t in order:
-        up, down = offsets[t]
+    for n in order:
+        _, _, up, down = items[n]
         if up != 0 or down != 0:
 
             @pl.when(inside(me, up, down, count))
-            def _(t=t):
-                remote(t).wait_send()
+            def _(n=n):
+                remote(n).wait_send()
 
     def orthonormal(out):
         gram = lax.dot_general(
@@ -243,18 +258,18 @@
     carry_out[...] = (projected[...] * jnp.sqrt(count / total)).astype(carry_out.dtype)
 
 
-def solve(theta, omega, count):
-    phys, capacity, width = theta.shape
+def solve(thetas, omega, count, phys):
+    _, capacity, width = thetas[0].shape
     rank = omega.shape[1]
     rows = phys * capacity
     vmem = pl.BlockSpec(memory_space=pltpu.VMEM)
     return pl.pallas_call(
-        functools.partial(solve_kernel, count),
+        functools.partial(solve_kernel, count, len(thetas) > 1, len(thetas)),
         out_shape=(
             jax.ShapeDtypeStruct((rows, rank), jnp.bfloat16),
             jax.ShapeDtypeStruct((rank, width), jnp.bfloat16),
         ),
-        in_specs=[pl.BlockSpec(memory_space=pl.ANY), vmem],
+        in_specs=[pl.BlockSpec(memory_space=pl.ANY)] * len(thetas) + [vmem],
         out_specs=(vmem, vmem),
         scratch_shapes=[
             pltpu.VMEM((rows, width), jnp.bfloat16),
@@ -274,15 +289,16 @@
             collective_id=0, has_side_effects=True, vmem_limit_bytes=40 * 1024 * 1024
         ),
         name="solve",
-    )(theta, omega)
+    )(*thetas, omega)
 
 
 def theta_kernel(carry, matrix, live, own, *rest):
     sites = (own,) + rest[:4]
     theta, parts, rows = rest[4:]
     width, capacity = carry.shape[0], carry.shape[1]
-    phys = theta.shape[0]
+    phys = own.shape[1] // capacity
     pairs = width * phys
+    outs = matrix.shape[0] // width
     pad = jnp.zeros((capacity, 128 - capacity % 128), own.dtype)
     for s in range(phys):
         for (first, last, _, _), source in zip(GROUPS, sites):
@@ -308,8 +324,8 @@
             )
             for k in range(2):
                 for v in range(width):
-                    rows[pl.ds(v * phys * capacity + a + k, phys, stride=capacity), :] = out[
-                        v * phys : (v + 1) * phys, k * 128 : (k + 1) * 128
+                    rows[pl.ds(v * outs * capacity + a + k, outs, stride=capacity), :] = out[
+                        v * outs : (v + 1) * outs, k * 128 : (k + 1) * 128
                     ]
         return 0
 
@@ -317,14 +333,14 @@
 
     def finish(t, _):
         pieces = [
-            rows[pl.ds(pl.multiple_of((v * phys + t) * capacity, 8), capacity), :][:, :capacity]
+            rows[pl.ds(pl.multiple_of((v * outs + t) * capacity, 8), capacity), :][:, :capacity]
             for v in range(width)
         ]
         joined = jnp.concatenate(pieces, 1)
         theta[t] = jnp.where(live[t] > 0.5, joined, 0.0).astype(theta.dtype)
         return 0
 
-    lax.fori_loop(0, phys, finish, 0)
+    lax.fori_loop(0, theta.shape[0], finish, 0)
 
 
 PITCH = 200
@@ -342,7 +358,7 @@
         out_specs=vmem,
         scratch_shapes=[
             pltpu.VMEM((PITCH * capacity, 128), jnp.float32),
-            pltpu.VMEM((width * phys * capacity, 128), jnp.float32),
+            pltpu.VMEM((matrix.shape[0] * capacity, 128), jnp.float32),
         ],
         compiler_params=pltpu.CompilerParams(vmem_limit_bytes=48 * 1024 * 1024),
         name="theta",
@@ -356,34 +372,65 @@
     bond_width = mpo.shape[0]
     phys_width = mpo.shape[1]
     raw = site[0]
-    sites = [raw] + [shifted(raw, "sec", up * GRID_DN + down) for _, _, up, down in GROUPS[1:]]
     phys_up, phys_down, bond_up, bond_down = charge_tables()
     rows = jnp.arange(capacity, dtype=jnp.int32)
-
-    def sizes_at(up, down):
-        at = jnp.clip(sector + jnp.asarray(up * GRID_DN + down), 0, count - 1)
-        hit = at[..., None] == jnp.arange(count, dtype=jnp.int32)
-        found = jnp.sum(jnp.where(hit, sector_sizes, 0), -1)
-        return jnp.where(inside(sector, up, down, count), found, 0)
-
-    own_size = sizes_at(np.zeros((1,), np.int32), np.zeros((1,), np.int32))
-    source_sizes = sizes_at(-bond_up, -bond_down)
-    carry_live = (rows[None, :, None] < own_size) & (
-        rows[None, None, :] < source_sizes[:, None, None]
-    )
-    carry_three = carry[0].reshape(capacity, bond_width, capacity).transpose(1, 0, 2)
-    carry_three = jnp.where(carry_live, carry_three, jnp.zeros_like(carry_three))
-    column_sizes = sizes_at(
-        phys_up[:, None] - bond_up[None, :], phys_down[:, None] - bond_down[None, :]
-    )
-    target_ok = inside(sector, phys_up, phys_down, count)
-    live = (rows[None, None, :] < column_sizes[:, :, None]) & target_ok[:, None, None]
-    live = live.astype(jnp.float32).reshape(phys_width, 1, bond_width * capacity)
+    paired = count == 2 * GRID_DN
     operator = jnp.where(jnp.asarray(conserving()), mpo, jnp.zeros_like(mpo))
-    pairs = phys_width * bond_width
-    matrix = operator.transpose(3, 1, 0, 2).reshape(pairs, pairs)
-    theta = make_theta(carry_three, matrix, live, sites)
-    left, next_carry = solve(theta, omega, count)
+
+    def theta_at(base, carry_block, sites, first, taken, padded):
+        def sizes_at(up, down):
+            at = jnp.clip(base + jnp.asarray(up * GRID_DN + down), 0, count - 1)
+            hit = at[..., None] == jnp.arange(count, dtype=jnp.int32)
+            found = jnp.sum(jnp.where(hit, sector_sizes, 0), -1)
+            return jnp.where(inside(base, up, down, count), found, 0)
+
+        own_size = sizes_at(np.zeros((1,), np.int32), np.zeros((1,), np.int32))
+        source_sizes = sizes_at(-bond_up, -bond_down)
+        carry_live = (rows[None, :, None] < own_size) & (
+            rows[None, None, :] < source_sizes[:, None, None]
+        )
+        carry_three = carry_block.reshape(capacity, bond_width, capacity).transpose(1, 0, 2)
+        carry_three = jnp.where(carry_live, carry_three, jnp.zeros_like(carry_three))
+        column_sizes = sizes_at(
+            phys_up[:, None] - bond_up[None, :], phys_down[:, None] - bond_down[None, :]
+        )
+        target_ok = inside(base, phys_up, phys_down, count)
+        live = (rows[None, None, :] < column_sizes[:, :, None]) & target_ok[:, None, None]
+        live = live.astype(jnp.float32).reshape(phys_width, 1, bond_width * capacity)
+        live = lax.dynamic_slice_in_dim(live, first, taken, 0)
+        used = lax.dynamic_slice_in_dim(operator, first, taken, 1)
+        used = jnp.pad(used, ((0, 0), (0, padded - taken), (0, 0), (0, 0)))
+        matrix = used.transpose(3, 1, 0, 2).reshape(
+            padded * bond_width, phys_width * bond_width
+        )
+        return make_theta(carry_three, matrix, live, sites)
+
+    if paired:
+        swap = [(i, (i + GRID_DN) % count) for i in range(count)]
+        other = lax.rem(sector + GRID_DN, count)
+        site_other = lax.ppermute(raw, "sec", swap)
+        carry_other = lax.ppermute(carry[0], "sec", swap)
+
+        def along(value, step):
+            moves = [
+                (i, i + step) for i in range(count) if 0 <= i % GRID_DN + step < GRID_DN
+            ]
+            return lax.ppermute(value, "sec", moves)
+
+        sites = [raw, site_other, site_other, along(raw, 1), along(raw, -1)]
+        others = [site_other, raw, raw, along(site_other, 1), along(site_other, -1)]
+        side = phys_width // 4
+        entry = (sector // GRID_DN) * (phys_width - side)
+        thetas = [
+            theta_at(sector, carry[0], sites, side, phys_width - 2 * side, phys_width - 2 * side),
+            theta_at(other, carry_other, others, entry, side, 2 * side),
+        ]
+    else:
+        sites = [raw] + [
+            shifted(raw, "sec", up * GRID_DN + down) for _, _, up, down in GROUPS[1:]
+        ]
+        thetas = [theta_at(sector, carry[0], sites, 0, phys_width, phys_width)]
+    left, next_carry = solve(thetas, omega, count, phys_width)
     return (left.reshape(1, phys_width, capacity, omega.shape[1]), next_carry[None])
 
 

time: 116 us -> 107 us (0.922)
  Pallas kernels: 90 us -> 67.7 us
  waiting for transfers between devices: 0.01 us -> 12.4 us
  other arithmetic: 8.17 us -> 4.64 us
  local copies, waits for them, and re-layouts: 4.23 us -> 5.87 us
  starting transfers between devices: 12.1 us -> 13.6 us
    pallas_call x1, Pallas kernels: 77.3 us -> 51.1 us  [solve(): pl.pallas_call(functools.partial(solve_kernel, count, len(thetas) > 1, le...]
    ppermute x4 -> x6, waiting for transfers between devices: 0.01 us -> 12.4 us  [the longest x1 11.9 us: body(): site_other = lax.ppermute(raw, 'sec', swap)]
    pallas_call x1 -> x2, Pallas kernels: 12.7 us -> 16.7 us  [make_theta(): pl.pallas_call(theta_kernel, out_shape=jax.ShapeDtypeStruct((phys, capaci...]
    ppermute x4 -> x6, starting transfers between devices: 12.1 us -> 13.6 us  [the longest x4 9.43 us: along(): return lax.ppermute(value, 'sec', moves)]
    transpose x1 -> x0, other arithmetic: 1.22 us -> none  [body(): matrix = operator.transpose(3, 1, 0, 2).reshape(pairs, pairs)]
    unnamed x7 -> x24, local copies, waits for them, and re-layouts: 2.62 us -> 2.75 us
  transfers between devices with their start and end apart: 4 -> 6, of which waited for: 0 -> 2; matrix products, arithmetic and copies ran while one was open for 9% -> 8% of each run, Pallas kernels for 0% -> 8%
where the time goes in v3:
time: 107 us
  Pallas kernels  67.7 us (63%)
  starting transfers between devices  13.6 us (13%)
  waiting for transfers between devices  12.4 us (12%)
  local copies, waits for them, and re-layouts  5.87 us (5%)
  other arithmetic  4.64 us (4%)
  between operations  2.41 us (2%)
    pallas_call x1, Pallas kernels, solve(): pl.pallas_call(functools.partial(solve_kernel, count, len(thetas) > 1, le...  51.1 us
    pallas_call x2, Pallas kernels, make_theta(): pl.pallas_call(theta_kernel, out_shape=jax.ShapeDtypeStruct((phys, capaci...  16.7 us
    ppermute x1, waiting for transfers between devices, body(): site_other = lax.ppermute(raw, 'sec', swap)  11.9 us
    ppermute x4, starting transfers between devices, along(): return lax.ppermute(value, 'sec', moves)  9.43 us
    ppermute x1, starting transfers between devices, body(): site_other = lax.ppermute(raw, 'sec', swap)  4.13 us
    unnamed x24, local copies, waits for them, and re-layouts  2.75 us
  transfers between devices with their start and end apart: 6, of which 2 were waited for; matrix products, arithmetic and copies ran while one was open for 8% of the time, Pallas kernels for 8%

profile of v3, /device:TPU:0, one launch (start us, length us, event | category | flops | bytes accessed | tf_op | source)
XLA Modules:
  0.0 106.7 jit_solution(13832239589395184616)
XLA Ops:
  0.7 1.4 %collective-permute-start.2 = (bf16[96,1536]{1,0:T(8,128)(2,1)}, bf16[96,1536]{1,0:T(8,128)(2,1)S(1)}, u32[]{:S(2)}, u32[]{:S(2)}) collective-permute-start(bf16[96,1536]{1,0:T(8,128)(2,1)} %bitcast.14), channel_id=1, source_target_pairs={{1,0},{2,1},{3,2},{4,3},{5,4},{6,5},{7,6},{9,8},{10,9},{11,10},{12... | collective-permute-start | bytes 884744 | tf_op jit(solution)/shard_map/ppermute | solution.py:418
  2.2 3.1 %collective-permute-start.1 = (bf16[96,1536]{1,0:T(8,128)(2,1)}, bf16[96,1536]{1,0:T(8,128)(2,1)S(1)}, u32[]{:S(2)}, u32[]{:S(2)}) collective-permute-start(bf16[96,1536]{1,0:T(8,128)(2,1)} %bitcast.15), channel_id=1, source_target_pairs={{0,1},{1,2},{2,3},{3,4},{4,5},{5,6},{6,7},{8,9},{9,10},{10,11},{11... | collective-permute-start | bytes 884744 | tf_op jit(solution)/shard_map/ppermute | solution.py:418
  5.2 4.1 %collective-permute-start = (bf16[96,1536]{1,0:T(8,128)(2,1)}, bf16[96,1536]{1,0:T(8,128)(2,1)S(1)}, u32[]{:S(2)}, u32[]{:S(2)}) collective-permute-start(bf16[96,1536]{1,0:T(8,128)(2,1)} %bitcast.16), channel_id=1, source_target_pairs={{0,8},{1,9},{2,10},{3,11},{4,12},{5,13},{6,14},{7,15},{8,0},{9,1},... | collective-permute-start | bytes 884744 | tf_op jit(solution)/shard_map/ppermute | solution.py:411
  9.4 1.1 %copy.48 = bf16[1,96,1152]{1,2,0:T(8,128)(2,1)S(1)} copy(bf16[1,96,1152]{2,1,0:T(8,128)(2,1)} %param.26) | data formatting | bytes 442368 | tf_op args[0]
  10.7 1.3 %fusion.11 = (s32[]{:T(128)}, s32[]{:T(128)}) fusion(s32[16]{0:T(128)} %param.30, s32[]{:T(128)S(6)} %min.43, s32[]{:T(128)S(6)} %min.42), kind=kLoop, calls=%fused_computation.44 | loop fusion | flops 94 | bytes 80 | tf_op jit(solution)/shard_map/reduce_sum | solution.py:384
  12.6 0.7 add_clamp_fusion.3
  13.3 1.2 %broadcast_select_fusion = bf16[12,16,16,12]{2,1,3,0:T(8,128)(2,1)S(1)} fusion(pred[12,16,16,12]{2,1,3,0:T(8,128)(4,1)} %constant.119.clone, bf16[12,16,16,12]{2,1,3,0:T(8,128)(2,1)} %param.28), kind=kLoop, calls=%fused_computation.4 | loop fusion | flops 36864 | bytes 184320 | tf_op jit(solution)/shard_map/jit(_where)/select_n | solution.py:378
  14.9 0.2 select_reduce_fusion.2
  15.3 0.6 select_reduce_fusion
  16.4 0.2 copy.49
  17.5 0.2 and_select_fusion.1.carry
  17.8 11.9 %collective-permute-done.rest_0_.rest_1_.own = bf16[96,1536]{1,0:T(8,128)(2,1)S(1)} collective-permute-done((bf16[96,1536]{1,0:T(8,128)(2,1)}, bf16[96,1536]{1,0:T(8,128)(2,1)S(1)}, u32[]{:S(2)}, u32[]{:S(2)}) %collective-permute-start) | collective-permute-done | bytes 294944 | tf_op jit(solution)/shard_map/ppermute | solution.py:411
  29.7 1.3 %collective-permute-start.5 = (bf16[96,1536]{1,0:T(8,128)(2,1)S(1)}, bf16[96,1536]{1,0:T(8,128)(2,1)S(1)}, u32[]{:S(2)}, u32[]{:S(2)}) collective-permute-start(bf16[96,1536]{1,0:T(8,128)(2,1)S(1)} %collective-permute-done.rest_0_.rest_1_.own), channel_id=1, source_target_pairs={{1,0},{2,1},{3,2},{4,3},{5,4},{6,5},{7,6},{9,8},{10,9},{11,10},{12... | collective-permute-start | bytes 884744 | tf_op jit(solution)/shard_map/ppermute | solution.py:418
  30.9 3.7 %collective-permute-start.4 = (bf16[96,1536]{1,0:T(8,128)(2,1)S(1)}, bf16[96,1536]{1,0:T(8,128)(2,1)S(1)}, u32[]{:S(2)}, u32[]{:S(2)}) collective-permute-start(bf16[96,1536]{1,0:T(8,128)(2,1)S(1)} %collective-permute-done.rest_0_.rest_1_.own), channel_id=1, source_target_pairs={{0,1},{1,2},{2,3},{3,4},{4,5},{5,6},{6,7},{8,9},{9,10},{10,11},{11... | collective-permute-start | bytes 884744 | tf_op jit(solution)/shard_map/ppermute | solution.py:418
  34.9 0.3 reshape.152.matrix
  35.3 0.3 reshape.154.matrix
  35.6 0.5 collective-permute-done.3
  36.1 1.1 %copy.54 = bf16[96,12,96]{2,0,1:T(8,128)(2,1)S(1)} copy(bf16[96,12,96]{0,2,1:T(8,128)(2,1)} %bitcast.5) | data formatting | bytes 442368 | tf_op jit(solution)/shard_map/reshape | solution.py:392
  37.2 0.2 and_select_fusion.carry
  37.4 8.6 %theta.2.refs_0_ = bf16[8,96,1152]{2,1,0:T(8,128)(2,1)S(1)} custom-call(bf16[12,96,96]{2,1,0:T(8,128)(2,1)S(1)} %and_select_fusion.1.carry, bf16[96,192]{1,0:T(8,128)(2,1)S(1)} %reshape.152.matrix, f32[8,1,1152]{2,1,0:T(1,128)S(1)} %reshape.195.live, bf16[96,1536]{1,0:T(8,128)(2,1)S(1)} %bitcast.17, ...), custom_call_target="tpu_custom_call" | custom-call | tf_op jit(solution)/shard_map/theta/pallas_call | solution.py:354
  46.1 8.1 %theta.3.refs_1_ = bf16[4,96,1152]{2,1,0:T(8,128)(2,1)S(1)} custom-call(bf16[12,96,96]{2,1,0:T(8,128)(2,1)S(1)} %and_select_fusion.carry, bf16[96,192]{1,0:T(8,128)(2,1)S(1)} %reshape.154.matrix, f32[4,1,1152]{2,1,0:T(1,128)S(1)} %and_convert_fusion.live, bf16[96,1536]{1,0:T(8,128)(2,1)S(1)} %collective-permute-done.rest_0_.rest_1_.own, ...), custom_call_target="tpu_custom_call" | custom-call | tf_op jit(solution)/shard_map/theta/pallas_call | solution.py:354
  54.2 51.1 %solve.1 = (bf16[1536,128]{1,0:T(8,128)(2,1)S(1)}, bf16[128,1152]{1,0:T(8,128)(2,1)S(1)}) custom-call(bf16[8,96,1152]{2,1,0:T(8,128)(2,1)S(1)} %theta.2.refs_0_, bf16[4,96,1152]{2,1,0:T(8,128)(2,1)S(1)} %theta.3.refs_1_, bf16[1152,128]{1,0:T(8,128)(2,1)S(1)} %copy-done.1), custom_call_target="tpu_custom_call" | custom-call | tf_op jit(solution)/shard_map/solve/pallas_call | solution.py:266
  105.2 0.7 copy.62
  106.0 0.7 copy.63
  (50 shorter events, 1.9 us)
Async XLA Ops:
  0.6 14.1 %copy-start.8 = (s32[16]{0:T(128)S(1)}, s32[16]{0:T(128)}, u32[]{:S(2)}) copy-start(s32[16]{0:T(128)} %constant.128.clone) | copy-start | bytes 196
  0.6 14.1 %copy-start.9 = (s32[16]{0:T(128)S(1)}, s32[16]{0:T(128)}, u32[]{:S(2)}) copy-start(s32[16]{0:T(128)} %constant.127.clone) | copy-start | bytes 196
  0.7 14.4 %copy-start.6 = (s32[12]{0:T(128)S(1)}, s32[12]{0:T(128)}, u32[]{:S(2)}) copy-start(s32[12]{0:T(128)} %constant.123.clone) | copy-start | bytes 148
  0.7 14.4 %copy-start.7 = (s32[12]{0:T(128)S(1)}, s32[12]{0:T(128)}, u32[]{:S(2)}) copy-start(s32[12]{0:T(128)} %constant.122.clone) | copy-start | bytes 148
  0.7 14.6 %copy-start.4 = (s32[16,12]{0,1:T(8,128)S(1)}, s32[16,12]{0,1:T(8,128)}, u32[]{:S(2)}) copy-start(s32[16,12]{0,1:T(8,128)} %constant.124.clone) | copy-start | bytes 2308
  0.7 15.2 %copy-start.2 = (s32[16,12]{0,1:T(8,128)S(1)}, s32[16,12]{0,1:T(8,128)}, u32[]{:S(2)}) copy-start(s32[16,12]{0,1:T(8,128)} %constant.126.clone) | copy-start | bytes 2308
  0.7 15.2 %copy-start.3 = (s32[16,12]{0,1:T(8,128)S(1)}, s32[16,12]{0,1:T(8,128)}, u32[]{:S(2)}) copy-start(s32[16,12]{0,1:T(8,128)} %constant.125.clone) | copy-start | bytes 2308
  0.7 14.2 %copy-start.5 = (s32[16]{0:T(128)S(1)}, s32[16]{0:T(128)}, u32[]{:S(2)}) copy-start(s32[16]{0:T(128)} %param.30) | copy-start | bytes 196
  0.7 36.7 %collective-permute-start.2 = (bf16[96,1536]{1,0:T(8,128)(2,1)}, bf16[96,1536]{1,0:T(8,128)(2,1)S(1)}, u32[]{:S(2)}, u32[]{:S(2)}) collective-permute-start(bf16[96,1536]{1,0:T(8,128)(2,1)} %bitcast.14), channel_id=1, source_target_pairs={{1,0},{2,1},{3,2},{4,3},{5,4},{6,5},{7,6},{9,8},{10,9},{11,10},{12... | collective-permute-start | bytes 884744 | tf_op jit(solution)/shard_map/ppermute | solution.py:418
  2.2 35.2 %collective-permute-start.1 = (bf16[96,1536]{1,0:T(8,128)(2,1)}, bf16[96,1536]{1,0:T(8,128)(2,1)S(1)}, u32[]{:S(2)}, u32[]{:S(2)}) collective-permute-start(bf16[96,1536]{1,0:T(8,128)(2,1)} %bitcast.15), channel_id=1, source_target_pairs={{0,1},{1,2},{2,3},{3,4},{4,5},{5,6},{6,7},{8,9},{9,10},{10,11},{11... | collective-permute-start | bytes 884744 | tf_op jit(solution)/shard_map/ppermute | solution.py:418
  5.2 24.4 %collective-permute-start = (bf16[96,1536]{1,0:T(8,128)(2,1)}, bf16[96,1536]{1,0:T(8,128)(2,1)S(1)}, u32[]{:S(2)}, u32[]{:S(2)}) collective-permute-start(bf16[96,1536]{1,0:T(8,128)(2,1)} %bitcast.16), channel_id=1, source_target_pairs={{0,8},{1,9},{2,10},{3,11},{4,12},{5,13},{6,14},{7,15},{8,0},{9,1},... | collective-permute-start | bytes 884744 | tf_op jit(solution)/shard_map/ppermute | solution.py:411
  10.5 25.6 %collective-permute-start.3 = (bf16[96,1152]{0,1:T(8,128)(2,1)S(1)}, bf16[96,1152]{0,1:T(8,128)(2,1)}, u32[]{:S(2)}, u32[]{:S(2)}) collective-permute-start(bf16[96,1152]{0,1:T(8,128)(2,1)S(1)} %bitcast.22), channel_id=1, source_target_pairs={{0,8},{1,9},{2,10},{3,11},{4,12},{5,13},{6,14},{7,15},{8,0},{9,1},... | collective-permute-start | bytes 663560 | tf_op jit(solution)/shard_map/ppermute | solution.py:412
  29.7 16.4 %collective-permute-start.5 = (bf16[96,1536]{1,0:T(8,128)(2,1)S(1)}, bf16[96,1536]{1,0:T(8,128)(2,1)S(1)}, u32[]{:S(2)}, u32[]{:S(2)}) collective-permute-start(bf16[96,1536]{1,0:T(8,128)(2,1)S(1)} %collective-permute-done.rest_0_.rest_1_.own), channel_id=1, source_target_pairs={{1,0},{2,1},{3,2},{4,3},{5,4},{6,5},{7,6},{9,8},{10,9},{11,10},{12... | collective-permute-start | bytes 884744 | tf_op jit(solution)/shard_map/ppermute | solution.py:418
  30.9 15.1 %collective-permute-start.4 = (bf16[96,1536]{1,0:T(8,128)(2,1)S(1)}, bf16[96,1536]{1,0:T(8,128)(2,1)S(1)}, u32[]{:S(2)}, u32[]{:S(2)}) collective-permute-start(bf16[96,1536]{1,0:T(8,128)(2,1)S(1)} %collective-permute-done.rest_0_.rest_1_.own), channel_id=1, source_target_pairs={{0,1},{1,2},{2,3},{3,4},{4,5},{5,6},{6,7},{8,9},{9,10},{10,11},{11... | collective-permute-start | bytes 884744 | tf_op jit(solution)/shard_map/ppermute | solution.py:418
  34.6 2.8 %copy-start = (bf16[1,96,1536]{2,1,0:T(8,128)(2,1)S(1)}, bf16[1,96,1536]{2,1,0:T(8,128)(2,1)}, u32[]{:S(2)}) copy-start(bf16[1,96,1536]{2,1,0:T(8,128)(2,1)} %param.27) | copy-start | bytes 884740
  46.0 8.1 %copy-start.1 = (bf16[1152,128]{1,0:T(8,128)(2,1)S(1)}, bf16[1152,128]{1,0:T(8,128)(2,1)}, u32[]{:S(2)}) copy-start(bf16[1152,128]{1,0:T(8,128)(2,1)} %refs_2_.1) | copy-start | bytes 884740
